TPU v7x, 32 devices: a whole 2x2x4 slice. The times are simulated.
32 devices in a mesh: seq: 8 (over y, x, core), dp: 4 (over z).
Axes of the slice: x: 2, y: 2, z: 4, core: 2. Of those that a mesh axis runs over, the one named last changes fastest.
Arguments:
- queries: bfloat16 [8, 512, 4096], P('dp', 'seq'), may hold values from -8 to 8
- unrotated_key_rows: bfloat16 [8, 512, 1024], P('dp', 'seq'), may hold values from -8 to 8
- value_projection_rows: bfloat16 [8, 512, 1024], P('dp', 'seq'), may hold values from -6 to 6
- attention_output_gradient: bfloat16 [8, 512, 4096], P('dp', 'seq'), may hold values from -16 to 16
- normed_hidden_input: bfloat16 [8, 512, 4096], P('dp', 'seq'), may hold values from -6 to 6
- adapter_down_weight: bfloat16 [4096, 64], replicated, may hold values from -0.01171875 to 0.01171875
- adapter_up_weight: bfloat16 [64, 4096], replicated, may hold values from -0.01171875 to 0.01171875
- lengths: int32 [8], P('dp'), may hold values from 256 to 512, as said below
- offsets: int32 [8], P('dp'), may hold values from 0 to 31
Outputs:
- grad_query: bfloat16 [8, 512, 4096], P('dp', 'seq')
- grad_key: bfloat16 [8, 512, 1024], P('dp', 'seq')
- grad_value: bfloat16 [8, 512, 1024], P('dp', 'seq')
- grad_down: float32 [4096, 64], P('seq')
- grad_up: float32 [64, 4096], P(None, 'seq')
Inputs may be any that keep to these rules, and one draw needn't show every extreme that they name: `lengths`: in every draw at least one rollout has all 512 positions valid.
All inputs are finite; a program needn't handle non-finite values.
Results may differ from a plain program's by a relative error of at most 0.018.
The roundings to bfloat16 on the way count: a program that leaves them out, or rounds other values in their place, can miss the bound.
Values may be sent and summed in bfloat16 or wider, within the bound.
A program may use at most 64 MiB of HBM per device.

v0:
```python
from functools import partial

import jax
import jax.numpy as jnp
from jax import lax
from jax.experimental import pallas as pl
from jax.experimental.pallas import tpu as pltpu
from jax.sharding import PartitionSpec as P

HEAD_WIDTH = 128


rotary_base = 500000.0


def partner_2(value, axis, distance):
    mask = 2**distance
    pairs = [(source, source ^ mask) for source in range(lax.axis_size(axis))]
    return lax.ppermute(value, axis, pairs)


def rotary_tables(length, head_size):
    half_size = head_size // 2
    frequency = rotary_base ** (-(jnp.arange(half_size, dtype=jnp.float32) * 2.0 / head_size))
    angles = jnp.arange(length, dtype=jnp.float32)[:, None] * frequency[None, :]
    return (jnp.cos(angles), jnp.sin(angles))


def rotate(fields, cosine, sine_table, direction):
    half_size = fields.shape[-1] // 2
    first_half = fields[..., :half_size]
    second_half = fields[..., half_size:]
    cos_wide = cosine[:, None, :]
    sin_wide = direction * sine_table[:, None, :]
    return jnp.concatenate(
        [
            first_half * cos_wide - second_half * sin_wide,
            second_half * cos_wide + first_half * sin_wide,
        ],
        axis=-1,
    )


def contract_axes(first_operand, second_operand, first_axis, second_axis):
    return lax.dot_general(
        first_operand,
        second_operand,
        (((first_axis,), (second_axis,)), ((), ())),
        preferred_element_type=jnp.float32,
    )


def block_terms(rot_query, rot_key, value_head, grad_head, offset, begin_row, end_row, score_scale):
    row_index = jnp.arange(begin_row, end_row, dtype=jnp.int32)[:, None]
    col_index = jnp.arange(end_row, dtype=jnp.int32)[None, :]
    visible = (col_index == row_index) | (col_index >= offset) & (col_index <= row_index)
    query_block = rot_query[begin_row:end_row]
    grad_block = grad_head[begin_row:end_row]
    key_block = rot_key[:end_row]
    value_block = value_head[:end_row]
    scores = contract_axes(query_block, key_block, 1, 1) * score_scale
    row_max = jnp.max(jnp.where(visible, scores, -jnp.inf), axis=1, keepdims=True)
    row_total = jnp.sum(jnp.where(visible, jnp.exp(scores - row_max), 0.0), axis=1, keepdims=True)
    grad_prob = contract_axes(grad_block, value_block, 1, 1)
    probability = jnp.where(visible, jnp.exp(scores - row_max), 0.0) / row_total
    row_delta = jnp.sum(probability * grad_prob, axis=1, keepdims=True)
    prob_low = probability.astype(jnp.bfloat16)
    grad_score = (probability * (grad_prob - row_delta) * score_scale).astype(jnp.bfloat16)
    block_grad = jnp.dot(grad_score, key_block, preferred_element_type=jnp.float32)
    key_add = contract_axes(grad_score, query_block, 0, 0)
    value_add = contract_axes(prob_low, grad_block, 0, 0)
    return (block_grad, key_add, value_add)


def head_backward(rot_query, rot_key, value_head, grad_head, offset, block_rows):
    length = rot_query.shape[0]
    head_size = rot_query.shape[1]
    score_scale = head_size ** (-0.5)
    query_parts = []
    key_terms = []
    value_terms = []
    for block_index in range(length // block_rows):
        begin_row = block_index * block_rows
        end_row = begin_row + block_rows
        live_terms = partial(
            block_terms,
            rot_query,
            rot_key,
            value_head,
            grad_head,
            offset,
            begin_row,
            end_row,
            score_scale,
        )
        results = live_terms()
        block_grad, key_add, value_add = results
        query_parts.append(block_grad)
        key_terms.append(jnp.pad(key_add, ((0, length - end_row), (0, 0))))
        value_terms.append(jnp.pad(value_add, ((0, length - end_row), (0, 0))))
    key_accum = key_terms[0]
    value_accum = value_terms[0]
    for term_index in range(1, len(key_terms)):
        key_accum = key_accum + key_terms[term_index]
        value_accum = value_accum + value_terms[term_index]
    return (jnp.concatenate(query_parts, axis=0), key_accum, value_accum)


def arrange_rows(rows, share, part_rows, key_groups):
    rollout_count = rows.shape[0]
    split = rows.reshape(rollout_count, share, part_rows, key_groups, HEAD_WIDTH)
    return jnp.transpose(split, (0, 2, 3, 1, 4)).reshape(
        rollout_count, part_rows, key_groups * share, HEAD_WIDTH
    )


def join_group(paired, share, seq_parts, part_rows):
    my_index = lax.axis_index("seq")
    rollout_count = paired.shape[1]
    local_keys = paired.shape[3]
    joined = paired[None]
    for bit in range(share.bit_length() - 1):
        partner = partner_2(joined, "seq", bit)
        upper = my_index // (1 << bit) % 2
        joined = jnp.where(
            upper == 0,
            jnp.concatenate([joined, partner], axis=0),
            jnp.concatenate([partner, joined], axis=0),
        )
    ordered = joined.reshape(share, 2, rollout_count, seq_parts, part_rows, local_keys, HEAD_WIDTH)
    ordered = jnp.transpose(ordered, (1, 2, 3, 0, 4, 5, 6))
    return ordered.reshape(2, rollout_count, seq_parts * share * part_rows, local_keys, HEAD_WIDTH)


def reduce_group(partial_sums, share, seq_parts, part_rows):
    my_index = lax.axis_index("seq")
    rollout_count = partial_sums.shape[1]
    local_keys = partial_sums.shape[3]
    split = partial_sums.reshape(
        2, rollout_count, seq_parts, share, part_rows, local_keys, HEAD_WIDTH
    )
    split = jnp.transpose(split, (3, 0, 1, 2, 4, 5, 6))
    for bit in reversed(range(share.bit_length() - 1)):
        half = split.shape[0] // 2
        lower_half = split[:half]
        upper_half = split[half:]
        upper = my_index // (1 << bit) % 2
        keep = jnp.where(upper == 0, lower_half, upper_half)
        outgoing = jnp.where(upper == 0, upper_half, lower_half)
        split = keep + partner_2(outgoing.astype(jnp.bfloat16), "seq", bit).astype(outgoing.dtype)
    return split[0].reshape(2, rollout_count, seq_parts * part_rows, local_keys, HEAD_WIDTH)


def on_device(
    queries,
    unrotated_key_rows,
    value_projection_rows,
    attention_output_gradient,
    normed_hidden_input,
    adapter_down_weight,
    adapter_up_weight,
    lengths,
    offsets,
):
    rollout_count = queries.shape[0]
    tokens = queries.shape[1]
    seq_parts = lax.axis_size("seq")
    length = tokens * seq_parts
    query_width = queries.shape[2]
    head_count = query_width // HEAD_WIDTH
    key_groups = unrotated_key_rows.shape[2] // HEAD_WIDTH
    local_heads = head_count // seq_parts
    adapter_rank_size = adapter_down_weight.shape[1]
    share = max(1, seq_parts // key_groups)
    part_rows = tokens // share
    query_tokens = queries.reshape(rollout_count, tokens, head_count, HEAD_WIDTH)
    grad_tokens = attention_output_gradient.reshape(rollout_count, tokens, head_count, HEAD_WIDTH)
    key_arranged = arrange_rows(unrotated_key_rows, share, part_rows, key_groups)
    value_arranged = arrange_rows(value_projection_rows, share, part_rows, key_groups)
    query_heads, key_parted, value_parted, grad_heads = (
        lax.all_to_all(query_tokens, "seq", split_axis=2, concat_axis=1, tiled=True),
        lax.all_to_all(key_arranged, "seq", split_axis=2, concat_axis=1, tiled=True),
        lax.all_to_all(value_arranged, "seq", split_axis=2, concat_axis=1, tiled=True),
        lax.all_to_all(grad_tokens, "seq", split_axis=2, concat_axis=1, tiled=True),
    )
    paired = join_group(jnp.stack([key_parted, value_parted], axis=0), share, seq_parts, part_rows)
    key_heads = paired[0]
    value_heads = paired[1]
    local_keys = key_heads.shape[2]
    cosine, sine_table = rotary_tables(length, HEAD_WIDTH)
    positions = jnp.arange(length, dtype=jnp.int32)
    keep_mask = (positions[None, :] >= offsets[:, None]) & (positions[None, :] < lengths[:, None])
    grad_heads = jnp.where(keep_mask[:, :, None, None], grad_heads, jnp.zeros_like(grad_heads))
    rot_query = rotate(query_heads.astype(jnp.float32), cosine, sine_table, 1.0).astype(
        jnp.bfloat16
    )
    rot_key = rotate(key_heads.astype(jnp.float32), cosine, sine_table, 1.0).astype(jnp.bfloat16)
    block_rows = min(512, length)
    query_rolls = []
    key_rolls = []
    value_rolls = []
    for rollout_slot in range(rollout_count):
        query_list = []
        key_list = []
        value_list = []
        for head_slot in range(local_heads):
            key_slot = head_slot * local_keys // local_heads
            query_grad, key_grad, value_grad = head_backward(
                rot_query[rollout_slot, :, head_slot],
                rot_key[rollout_slot, :, key_slot],
                value_heads[rollout_slot, :, key_slot],
                grad_heads[rollout_slot, :, head_slot],
                offsets[rollout_slot],
                block_rows,
            )
            query_list.append(
                rotate(query_grad[:, None, :], cosine, sine_table, -1.0)[:, 0].astype(jnp.bfloat16)
            )
            key_list.append(
                rotate(key_grad[:, None, :], cosine, sine_table, -1.0)[:, 0].astype(jnp.bfloat16)
            )
            value_list.append(value_grad.astype(jnp.bfloat16))
        query_rolls.append(jnp.stack(query_list, axis=1))
        key_rolls.append(jnp.stack(key_list, axis=1))
        value_rolls.append(jnp.stack(value_list, axis=1))
    query_back = jnp.stack(query_rolls, axis=0)
    key_parts = jnp.stack(key_rolls, axis=0)
    value_parts = jnp.stack(value_rolls, axis=0)
    shared_heads = local_heads // local_keys
    key_local = (
        key_parts.astype(jnp.float32)
        .reshape(rollout_count, length, local_keys, shared_heads, HEAD_WIDTH)
        .sum(axis=3)
    )
    value_local = (
        value_parts.astype(jnp.float32)
        .reshape(rollout_count, length, local_keys, shared_heads, HEAD_WIDTH)
        .sum(axis=3)
    )
    summed = reduce_group(
        jnp.stack([key_local, value_local], axis=0), share, seq_parts, part_rows
    ).astype(jnp.bfloat16)
    query_result, key_result, value_result = (
        lax.all_to_all(query_back, "seq", split_axis=1, concat_axis=2, tiled=True),
        lax.all_to_all(summed[0], "seq", split_axis=1, concat_axis=2, tiled=True),
        lax.all_to_all(summed[1], "seq", split_axis=1, concat_axis=2, tiled=True),
    )
    key_total = jnp.transpose(
        key_result.reshape(rollout_count, part_rows, key_groups, share, HEAD_WIDTH), (0, 3, 1, 2, 4)
    ).reshape(rollout_count, tokens, key_groups * HEAD_WIDTH)
    value_total = jnp.transpose(
        value_result.reshape(rollout_count, part_rows, key_groups, share, HEAD_WIDTH),
        (0, 3, 1, 2, 4),
    ).reshape(rollout_count, tokens, key_groups * HEAD_WIDTH)
    flattened_query = query_result.reshape(rollout_count * tokens, query_width)
    hidden_state = normed_hidden_input.reshape(rollout_count * tokens, normed_hidden_input.shape[2])
    adapter_latent = jnp.dot(
        hidden_state, adapter_down_weight, preferred_element_type=jnp.float32
    ).astype(jnp.bfloat16)
    backward_gradient = contract_axes(flattened_query, adapter_up_weight, 1, 1).astype(jnp.bfloat16)
    joined_terms = lax.psum_scatter(
        jnp.concatenate(
            [
                contract_axes(hidden_state, backward_gradient, 0, 0),
                contract_axes(flattened_query, adapter_latent, 0, 0),
            ],
            axis=1,
        ).astype(jnp.bfloat16),
        "seq",
        scatter_dimension=0,
        tiled=True,
    ).astype(jnp.float32)
    down_local = joined_terms[:, :adapter_rank_size]
    up_local = joined_terms[:, adapter_rank_size:]
    down_sum, up_sum = (
        lax.psum(down_local.astype(jnp.bfloat16), "dp").astype(jnp.float32),
        lax.psum(up_local.astype(jnp.bfloat16), "dp").astype(jnp.float32),
    )
    return (
        flattened_query.reshape(rollout_count, tokens, query_width),
        key_total,
        value_total,
        down_sum,
        up_sum.T,
    )


CHUNKS = 4
VMEM_BUDGET = 44 * 1024 * 1024
NEG = -1e30


def nt_dot(left, right):
    return lax.dot_general(
        left, right, (((1,), (1,)), ((), ())), preferred_element_type=jnp.float32
    )


def subsets(bits):
    masks = [0]
    for bit in bits:
        masks = masks + [mask | (1 << bit) for mask in masks]
    return masks


def fused_kernel(
    n_seq,
    n_dp,
    n_roll,
    tokens,
    kv_heads,
    group,
    rank,
    chunks,
    off_ref,
    len_ref,
    cos_ref,
    sin_ref,
    q_ref,
    k_ref,
    v_ref,
    g_ref,
    hid_ref,
    down_ref,
    up_ref,
    gq_ref,
    gk_ref,
    gv_ref,
    gd_ref,
    gu_ref,
    kv_all,
    dkv,
    red_buf,
    ad_buf,
    ad_red,
    dp_buf,
    ag_send,
    ag_recv,
    rs_send,
    rs_recv,
    ad_send,
    ad_recv,
    dp_send,
    dp_recv,
):
    me = lax.axis_index("seq")
    my_dp = lax.axis_index("dp")
    n_bits = n_seq.bit_length() - 1
    chip_bits = list(range(1, n_bits))
    gather_orders = [chip_bits + [0], chip_bits[::-1] + [0]]
    reduce_orders = [[0] + chip_bits[::-1], [0] + chip_bits]
    heads_per = kv_heads // chunks
    width = HEAD_WIDTH
    rows = group * tokens
    length = n_seq * tokens
    scale = width ** (-0.5)
    cols = q_ref.shape[1] // n_seq
    pending = []

    barrier = pltpu.get_barrier_semaphore()
    for bit in range(n_bits):
        pl.semaphore_signal(barrier, inc=1, device_id={"seq": me ^ (1 << bit)})
    for step in range(1, n_dp):
        pl.semaphore_signal(barrier, inc=1, device_id={"dp": lax.rem(my_dp + step, n_dp)})

    cos = cos_ref[...]
    sin = sin_ref[...]

    def slot_rows(mask):
        return pl.ds(pl.multiple_of((me ^ mask) * tokens, tokens), tokens)

    def load_chunk(c):
        for h in range(c * heads_per, (c + 1) * heads_per):
            for r in range(n_roll):
                span = slice(r * tokens, (r + 1) * tokens)
                lane = slice(h * width, (h + 1) * width)
                key = k_ref[span, lane].astype(jnp.float32)
                key = key * cos + pltpu.roll(key, width // 2, 1) * sin
                kv_all[0, h, r, slot_rows(0), :] = key.astype(jnp.bfloat16)
                kv_all[1, h, r, slot_rows(0), :] = v_ref[span, lane]

    gather_ops = {}

    def gather_send(c, stage):
        for t in range(2):
            order = gather_orders[t]
            bit = order[stage]
            for mask in subsets(order[:stage]):
                block = kv_all.at[
                    t, pl.ds(c * heads_per, heads_per), slice(None), slot_rows(mask), slice(None)
                ]
                got = mask | (1 << bit)
                copy = pltpu.make_async_remote_copy(
                    src_ref=block,
                    dst_ref=block,
                    send_sem=ag_send.at[t, c, got],
                    recv_sem=ag_recv.at[t, c, got],
                    device_id={"seq": me ^ (1 << bit)},
                )
                copy.start()
                gather_ops.setdefault((c, stage), []).append(copy)
                pending.append(copy)

    def gather_wait(c, stage):
        for copy in gather_ops[(c, stage)]:
            copy.wait_recv()

    reduce_ops = {}

    def reduce_send(c, stage):
        for t in range(2):
            order = reduce_orders[t]
            bit = order[stage]
            for rest in subsets(order[stage + 1 :]):
                mask = rest | (1 << bit)
                head_span = pl.ds(c * heads_per, heads_per)
                copy = pltpu.make_async_remote_copy(
                    src_ref=dkv.at[t, head_span, slice(None), slot_rows(mask), slice(None)],
                    dst_ref=red_buf.at[t, mask, head_span],
                    send_sem=rs_send.at[t, c, mask],
                    recv_sem=rs_recv.at[t, c, mask],
                    device_id={"seq": me ^ (1 << bit)},
                )
                copy.start()
                reduce_ops.setdefault((c, stage), []).append((t, mask, rest, copy))
                pending.append(copy)

    def reduce_add(c, stage):
        for t, mask, rest, copy in reduce_ops[(c, stage)]:
            copy.wait_recv()
            for h in range(c * heads_per, (c + 1) * heads_per):
                for r in range(n_roll):
                    total = dkv[t, h, r, slot_rows(rest), :].astype(jnp.float32)
                    total = total + red_buf[t, mask, h, r].astype(jnp.float32)
                    if stage < n_bits - 1:
                        dkv[t, h, r, slot_rows(rest), :] = total.astype(jnp.bfloat16)
                        continue
                    span = slice(r * tokens, (r + 1) * tokens)
                    lane = slice(h * width, (h + 1) * width)
                    if t == 0:
                        total = total * cos - pltpu.roll(total, width // 2, 1) * sin
                        gk_ref[span, lane] = total.astype(jnp.bfloat16)
                    else:
                        gv_ref[span, lane] = total.astype(jnp.bfloat16)

    def advance_reduce(c, stage):
        if stage > 0:
            reduce_add(c, stage - 1)
        if stage < n_bits:
            reduce_send(c, stage)

    adapter_ops = {}

    def adapter_send(stage):
        for t in range(2):
            order = reduce_orders[t]
            bit = order[stage]
            for rest in subsets(order[stage + 1 :]):
                mask = rest | (1 << bit)
                copy = pltpu.make_async_remote_copy(
                    src_ref=ad_buf.at[t, me ^ mask],
                    dst_ref=ad_red.at[t, mask],
                    send_sem=ad_send.at[t, mask],
                    recv_sem=ad_recv.at[t, mask],
                    device_id={"seq": me ^ (1 << bit)},
                )
                copy.start()
                adapter_ops.setdefault(stage, []).append((t, mask, rest, copy))
                pending.append(copy)

    def adapter_add(stage):
        for t, mask, rest, copy in adapter_ops[stage]:
            copy.wait_recv()
            total = ad_buf[t, me ^ rest].astype(jnp.float32) + ad_red[t, mask].astype(jnp.float32)
            total = total.astype(jnp.bfloat16)
            if stage < n_bits - 1:
                ad_buf[t, me ^ rest] = total
            else:
                dp_buf[my_dp, t] = total

    def advance_adapter(stage):
        if stage > 0:
            adapter_add(stage - 1)
        if stage < n_bits:
            adapter_send(stage)

    key_index = lax.broadcasted_iota(jnp.int32, (length, rows), 0)
    row_index = me * tokens + lax.broadcasted_iota(jnp.int32, (1, rows), 1) % tokens
    token_index = me * tokens + lax.broadcasted_iota(jnp.int32, (tokens, width), 0)

    def pair_work(c, index):
        h = c * heads_per + index // n_roll
        r = index % n_roll
        span = pl.ds(pl.multiple_of(r * tokens, tokens), tokens)
        offset = off_ref[r]
        keep = (token_index >= offset) & (token_index < len_ref[r])
        queries = []
        grads = []
        for j in range(group):
            lane = pl.ds(pl.multiple_of((h * group + j) * width, width), width)
            query = q_ref[span, lane].astype(jnp.float32)
            query = query * cos + pltpu.roll(query, width // 2, 1) * sin
            queries.append(query.astype(jnp.bfloat16))
            grad = g_ref[span, lane].astype(jnp.float32)
            grads.append(jnp.where(keep, grad, 0.0).astype(jnp.bfloat16))
        query = jnp.concatenate(queries, axis=0)
        grad = jnp.concatenate(grads, axis=0)
        key = kv_all[0, h, r]
        value = kv_all[1, h, r]
        visible = (key_index == row_index) | ((key_index >= offset) & (key_index <= row_index))
        scores = jnp.where(visible, nt_dot(key, query) * scale, NEG)
        weights = jnp.exp(scores - jnp.max(scores, axis=0, keepdims=True))
        prob = weights * (1.0 / jnp.sum(weights, axis=0, keepdims=True))
        grad_prob = nt_dot(value, grad)
        delta = jnp.sum(prob * grad_prob, axis=0, keepdims=True)
        grad_score = (prob * (grad_prob - delta) * scale).astype(jnp.bfloat16)
        prob_low = prob.astype(jnp.bfloat16)
        dkv[1, h, r] = jnp.dot(prob_low, grad, preferred_element_type=jnp.float32).astype(
            jnp.bfloat16
        )
        dkv[0, h, r] = jnp.dot(grad_score, query, preferred_element_type=jnp.float32).astype(
            jnp.bfloat16
        )
        back = jnp.dot(key.T, grad_score, preferred_element_type=jnp.float32).T
        for j in range(group):
            lane = pl.ds(pl.multiple_of((h * group + j) * width, width), width)
            part = back[j * tokens : (j + 1) * tokens]
            part = part * cos - pltpu.roll(part, width // 2, 1) * sin
            gq_ref[span, lane] = part.astype(jnp.bfloat16)

    def compute_chunk(c):
        def body(index, carry):
            pair_work(c, index)
            return carry

        lax.fori_loop(0, heads_per * n_roll, body, 0)

    load_chunk(0)
    pl.semaphore_wait(barrier, n_bits + n_dp - 1)
    latent = None
    for slot in range(chunks + 2 * n_bits + 1):
        for c in range(chunks):
            stage = slot - c
            if stage == 0 and c > 0:
                load_chunk(c)
            if 0 < stage <= n_bits:
                gather_wait(c, stage - 1)
            if 0 <= stage < n_bits:
                gather_send(c, stage)
        for c in range(chunks):
            stage = slot - c - n_bits
            if 1 <= stage <= n_bits:
                advance_reduce(c, stage)
        if slot == 0:
            latent = nt_dot(down_ref[...], hid_ref[...]).astype(jnp.bfloat16)
        ready = slot - n_bits
        if 0 <= ready < chunks:
            compute_chunk(ready)
            advance_reduce(ready, 0)
        if ready == chunks - 1:
            back = nt_dot(up_ref[...], gq_ref[...]).astype(jnp.bfloat16)
            for d in range(n_seq):
                lane = slice(d * cols, (d + 1) * cols)
                ad_buf[0, d] = jnp.dot(
                    back, hid_ref[:, lane], preferred_element_type=jnp.float32
                ).astype(jnp.bfloat16)
                ad_buf[1, d] = jnp.dot(
                    latent, gq_ref[:, lane], preferred_element_type=jnp.float32
                ).astype(jnp.bfloat16)
            advance_adapter(0)
        elif chunks <= ready < chunks + n_bits:
            advance_adapter(ready - chunks + 1)

    dp_ops = []
    for step in range(1, n_dp):
        copy = pltpu.make_async_remote_copy(
            src_ref=dp_buf.at[my_dp],
            dst_ref=dp_buf.at[my_dp],
            send_sem=dp_send.at[step],
            recv_sem=dp_recv.at[step],
            device_id={"dp": lax.rem(my_dp + step, n_dp)},
        )
        copy.start()
        dp_ops.append(copy)
        pending.append(copy)
    for copy in dp_ops:
        copy.wait_recv()
    down_total = dp_buf[0, 0].astype(jnp.float32)
    up_total = dp_buf[0, 1].astype(jnp.float32)
    for d in range(1, n_dp):
        down_total = down_total + dp_buf[d, 0].astype(jnp.float32)
        up_total = up_total + dp_buf[d, 1].astype(jnp.float32)
    gd_ref[...] = down_total
    gu_ref[...] = up_total
    for copy in pending:
        copy.wait_send()


def fused_on_device(
    n_seq,
    n_dp,
    queries,
    unrotated_key_rows,
    value_projection_rows,
    attention_output_gradient,
    normed_hidden_input,
    adapter_down_weight,
    adapter_up_weight,
    lengths,
    offsets,
):
    n_roll, tokens, q_width = queries.shape
    kv_width = unrotated_key_rows.shape[2]
    kv_heads = kv_width // HEAD_WIDTH
    group = q_width // kv_width
    rank = adapter_down_weight.shape[1]
    chunks = min(CHUNKS, kv_heads)
    flat = n_roll * tokens
    half = HEAD_WIDTH // 2
    frequency = rotary_base ** (-(jnp.arange(half, dtype=jnp.float32) * 2.0 / HEAD_WIDTH))
    positions = lax.axis_index("seq") * tokens + jnp.arange(tokens, dtype=jnp.int32)
    angles = positions.astype(jnp.float32)[:, None] * frequency[None, :]
    cosine, sine = jnp.cos(angles), jnp.sin(angles)
    cos_wide = jnp.concatenate([cosine, cosine], axis=1)
    sin_wide = jnp.concatenate([-sine, sine], axis=1)
    vmem = pl.BlockSpec(memory_space=pltpu.VMEM)
    smem = pl.BlockSpec(memory_space=pltpu.SMEM)
    cols = q_width // n_seq
    low = jnp.bfloat16
    dma = pltpu.SemaphoreType.DMA
    outs = pl.pallas_call(
        partial(fused_kernel, n_seq, n_dp, n_roll, tokens, kv_heads, group, rank, chunks),
        out_shape=(
            jax.ShapeDtypeStruct((flat, q_width), low),
            jax.ShapeDtypeStruct((flat, kv_width), low),
            jax.ShapeDtypeStruct((flat, kv_width), low),
            jax.ShapeDtypeStruct((rank, cols), jnp.float32),
            jax.ShapeDtypeStruct((rank, cols), jnp.float32),
        ),
        in_specs=[smem, smem] + [vmem] * 9,
        out_specs=[vmem] * 5,
        scratch_shapes=[
            pltpu.VMEM((2, kv_heads, n_roll, n_seq * tokens, HEAD_WIDTH), low),
            pltpu.VMEM((2, kv_heads, n_roll, n_seq * tokens, HEAD_WIDTH), low),
            pltpu.VMEM((2, n_seq, kv_heads, n_roll, tokens, HEAD_WIDTH), low),
            pltpu.VMEM((2, n_seq, rank, cols), low),
            pltpu.VMEM((2, n_seq, rank, cols), low),
            pltpu.VMEM((n_dp, 2, rank, cols), low),
            dma((2, chunks, n_seq)),
            dma((2, chunks, n_seq)),
            dma((2, chunks, n_seq)),
            dma((2, chunks, n_seq)),
            dma((2, n_seq)),
            dma((2, n_seq)),
            dma((n_dp,)),
            dma((n_dp,)),
        ],
        compiler_params=pltpu.CompilerParams(
            collective_id=0, has_side_effects=True, vmem_limit_bytes=60 * 1024 * 1024
        ),
    )(
        offsets,
        lengths,
        cos_wide,
        sin_wide,
        queries.reshape(flat, q_width),
        unrotated_key_rows.reshape(flat, kv_width),
        value_projection_rows.reshape(flat, kv_width),
        attention_output_gradient.reshape(flat, q_width),
        normed_hidden_input.reshape(flat, q_width),
        adapter_down_weight.T,
        adapter_up_weight,
    )
    grad_query, grad_key, grad_value, grad_down, grad_up = outs
    return (
        grad_query.reshape(n_roll, tokens, q_width),
        grad_key.reshape(n_roll, tokens, kv_width),
        grad_value.reshape(n_roll, tokens, kv_width),
        grad_down.T,
        grad_up,
    )


def dispatch(mesh, *args):
    n_seq = mesh.shape["seq"]
    n_roll, tokens, q_width = args[0].shape
    kv_width = args[1].shape[2]
    gathered = 2 * n_roll * n_seq * tokens * kv_width * 2
    if 3 * gathered + 7 * n_roll * tokens * q_width * 2 > VMEM_BUDGET:
        return on_device(*args)
    return fused_on_device(n_seq, mesh.shape["dp"], *args)


def solution(mesh):
    in_specs = (
        P("dp", "seq", None),
        P("dp", "seq", None),
        P("dp", "seq", None),
        P("dp", "seq", None),
        P("dp", "seq", None),
        P(),
        P(),
        P("dp"),
        P("dp"),
    )
    out_specs = (
        P("dp", "seq", None),
        P("dp", "seq", None),
        P("dp", "seq", None),
        P("seq", None),
        P(None, "seq"),
    )
    return jax.shard_map(
        partial(dispatch, mesh), mesh=mesh, in_specs=in_specs, out_specs=out_specs, check_vma=False
    )
```

profile of v0, /device:TPU:0, one launch (start us, length us, event | category | flops | bytes accessed | tf_op | source)
XLA Modules:
  0.0 81.4 jit_solution(11942308575766145727)
XLA Ops:
  0.7 0.2 fusion
  0.9 0.7 pad_maximum_fusion
  1.6 73.9 %shard_map.128 = (bf16[128,4096]{1,0:T(8,128)(2,1)}, bf16[128,1024]{1,0:T(8,128)(2,1)}, bf16[128,1024]{1,0:T(8,128)(2,1)}, f32[64,512]{1,0:T(8,128)}, f32[64,512]{1,0:T(8,128)}) custom-call(s32[2]{0:T(128)} %off_ref.1, s32[2]{0:T(128)} %len_ref.1, f32[64,128]{1,0:T(8,128)} %get-tuple-element.18.cos_ref, f32[64,128]{1,0:T(8,128)} %get-tuple-element.19.sin_ref, ...), custom_call_target="tpu_custom_call" | custom-call | tf_op jit(solution)/shard_map/pallas_call | solution.py:631
  75.4 0.0 copy-start.1
  75.5 2.3 %copy.19 = bf16[2,64,4096]{2,1,0:T(8,128)(2,1)} copy(bf16[2,64,4096]{2,1,0:T(8,128)(2,1)} %bitcast.10) | data formatting | bytes 2097152
  77.8 0.0 copy-done.1
  77.8 0.0 copy-start
  77.8 0.7 copy.20
  78.5 0.3 copy-done
  78.8 0.0 copy-start.3
  78.8 0.7 copy.21
  79.5 0.3 copy-done.3
  79.8 0.0 copy-start.2
  79.8 0.7 copy.22
  80.5 0.3 copy-done.2
  80.8 0.7 copy.23
  (2 shorter events, 0.0 us)
Async XLA Ops:
  75.4 2.3 %copy-start.1 = (bf16[128,1024]{1,0:T(8,128)(2,1)S(1)}, bf16[128,1024]{1,0:T(8,128)(2,1)}, u32[]{:S(2)}) copy-start(bf16[128,1024]{1,0:T(8,128)(2,1)} %get-tuple-element.11) | copy-start | bytes 786436
  77.8 1.0 %copy-start = (bf16[128,1024]{1,0:T(8,128)(2,1)S(1)}, bf16[128,1024]{1,0:T(8,128)(2,1)}, u32[]{:S(2)}) copy-start(bf16[128,1024]{1,0:T(8,128)(2,1)} %get-tuple-element.12) | copy-start | bytes 786436
  78.8 1.0 %copy-start.3 = (f32[64,512]{1,0:T(8,128)S(1)}, f32[64,512]{1,0:T(8,128)}, u32[]{:S(2)}) copy-start(f32[64,512]{1,0:T(8,128)} %get-tuple-element.13) | copy-start | bytes 393220
  79.8 1.0 %copy-start.2 = (f32[64,512]{1,0:T(8,128)S(1)}, f32[64,512]{1,0:T(8,128)}, u32[]{:S(2)}) copy-start(f32[64,512]{1,0:T(8,128)} %get-tuple-element.29) | copy-start | bytes 393220
where the time goes:
time: 81.7 us; the launch traced here: 81.4 us
  Pallas kernels  73.9 us (90%)
  local copies, waits for them, and re-layouts  5.98 us (7%)
  other arithmetic  0.93 us (1%)
    pallas_call x1, Pallas kernels, fused_on_device(): pl.pallas_call(partial(fused_kernel, n_seq, n_dp, n_roll, tokens, kv_head...  73.9 us
    unnamed x13, local copies, waits for them, and re-layouts  5.98 us

commit v1 on v0

v1 whole, which is shorter than its diff:
```python
from functools import partial

import math

import jax
import jax.numpy as jnp
import numpy as np
from jax import lax
from jax.experimental import pallas as pl
from jax.experimental.pallas import tpu as pltpu
from jax.sharding import PartitionSpec as P

HEAD_WIDTH = 128


rotary_base = 500000.0


def partner_2(value, axis, distance):
    mask = 2**distance
    pairs = [(source, source ^ mask) for source in range(lax.axis_size(axis))]
    return lax.ppermute(value, axis, pairs)


def rotary_tables(length, head_size):
    half_size = head_size // 2
    frequency = rotary_base ** (-(jnp.arange(half_size, dtype=jnp.float32) * 2.0 / head_size))
    angles = jnp.arange(length, dtype=jnp.float32)[:, None] * frequency[None, :]
    return (jnp.cos(angles), jnp.sin(angles))


def rotate(fields, cosine, sine_table, direction):
    half_size = fields.shape[-1] // 2
    first_half = fields[..., :half_size]
    second_half = fields[..., half_size:]
    cos_wide = cosine[:, None, :]
    sin_wide = direction * sine_table[:, None, :]
    return jnp.concatenate(
        [
            first_half * cos_wide - second_half * sin_wide,
            second_half * cos_wide + first_half * sin_wide,
        ],
        axis=-1,
    )


def contract_axes(first_operand, second_operand, first_axis, second_axis):
    return lax.dot_general(
        first_operand,
        second_operand,
        (((first_axis,), (second_axis,)), ((), ())),
        preferred_element_type=jnp.float32,
    )


def block_terms(rot_query, rot_key, value_head, grad_head, offset, begin_row, end_row, score_scale):
    row_index = jnp.arange(begin_row, end_row, dtype=jnp.int32)[:, None]
    col_index = jnp.arange(end_row, dtype=jnp.int32)[None, :]
    visible = (col_index == row_index) | (col_index >= offset) & (col_index <= row_index)
    query_block = rot_query[begin_row:end_row]
    grad_block = grad_head[begin_row:end_row]
    key_block = rot_key[:end_row]
    value_block = value_head[:end_row]
    scores = contract_axes(query_block, key_block, 1, 1) * score_scale
    row_max = jnp.max(jnp.where(visible, scores, -jnp.inf), axis=1, keepdims=True)
    row_total = jnp.sum(jnp.where(visible, jnp.exp(scores - row_max), 0.0), axis=1, keepdims=True)
    grad_prob = contract_axes(grad_block, value_block, 1, 1)
    probability = jnp.where(visible, jnp.exp(scores - row_max), 0.0) / row_total
    row_delta = jnp.sum(probability * grad_prob, axis=1, keepdims=True)
    prob_low = probability.astype(jnp.bfloat16)
    grad_score = (probability * (grad_prob - row_delta) * score_scale).astype(jnp.bfloat16)
    block_grad = jnp.dot(grad_score, key_block, preferred_element_type=jnp.float32)
    key_add = contract_axes(grad_score, query_block, 0, 0)
    value_add = contract_axes(prob_low, grad_block, 0, 0)
    return (block_grad, key_add, value_add)


def head_backward(rot_query, rot_key, value_head, grad_head, offset, block_rows):
    length = rot_query.shape[0]
    head_size = rot_query.shape[1]
    score_scale = head_size ** (-0.5)
    query_parts = []
    key_terms = []
    value_terms = []
    for block_index in range(length // block_rows):
        begin_row = block_index * block_rows
        end_row = begin_row + block_rows
        live_terms = partial(
            block_terms,
            rot_query,
            rot_key,
            value_head,
            grad_head,
            offset,
            begin_row,
            end_row,
            score_scale,
        )
        results = live_terms()
        block_grad, key_add, value_add = results
        query_parts.append(block_grad)
        key_terms.append(jnp.pad(key_add, ((0, length - end_row), (0, 0))))
        value_terms.append(jnp.pad(value_add, ((0, length - end_row), (0, 0))))
    key_accum = key_terms[0]
    value_accum = value_terms[0]
    for term_index in range(1, len(key_terms)):
        key_accum = key_accum + key_terms[term_index]
        value_accum = value_accum + value_terms[term_index]
    return (jnp.concatenate(query_parts, axis=0), key_accum, value_accum)


def arrange_rows(rows, share, part_rows, key_groups):
    rollout_count = rows.shape[0]
    split = rows.reshape(rollout_count, share, part_rows, key_groups, HEAD_WIDTH)
    return jnp.transpose(split, (0, 2, 3, 1, 4)).reshape(
        rollout_count, part_rows, key_groups * share, HEAD_WIDTH
    )


def join_group(paired, share, seq_parts, part_rows):
    my_index = lax.axis_index("seq")
    rollout_count = paired.shape[1]
    local_keys = paired.shape[3]
    joined = paired[None]
    for bit in range(share.bit_length() - 1):
        partner = partner_2(joined, "seq", bit)
        upper = my_index // (1 << bit) % 2
        joined = jnp.where(
            upper == 0,
            jnp.concatenate([joined, partner], axis=0),
            jnp.concatenate([partner, joined], axis=0),
        )
    ordered = joined.reshape(share, 2, rollout_count, seq_parts, part_rows, local_keys, HEAD_WIDTH)
    ordered = jnp.transpose(ordered, (1, 2, 3, 0, 4, 5, 6))
    return ordered.reshape(2, rollout_count, seq_parts * share * part_rows, local_keys, HEAD_WIDTH)


def reduce_group(partial_sums, share, seq_parts, part_rows):
    my_index = lax.axis_index("seq")
    rollout_count = partial_sums.shape[1]
    local_keys = partial_sums.shape[3]
    split = partial_sums.reshape(
        2, rollout_count, seq_parts, share, part_rows, local_keys, HEAD_WIDTH
    )
    split = jnp.transpose(split, (3, 0, 1, 2, 4, 5, 6))
    for bit in reversed(range(share.bit_length() - 1)):
        half = split.shape[0] // 2
        lower_half = split[:half]
        upper_half = split[half:]
        upper = my_index // (1 << bit) % 2
        keep = jnp.where(upper == 0, lower_half, upper_half)
        outgoing = jnp.where(upper == 0, upper_half, lower_half)
        split = keep + partner_2(outgoing.astype(jnp.bfloat16), "seq", bit).astype(outgoing.dtype)
    return split[0].reshape(2, rollout_count, seq_parts * part_rows, local_keys, HEAD_WIDTH)


def on_device(
    queries,
    unrotated_key_rows,
    value_projection_rows,
    attention_output_gradient,
    normed_hidden_input,
    adapter_down_weight,
    adapter_up_weight,
    lengths,
    offsets,
):
    rollout_count = queries.shape[0]
    tokens = queries.shape[1]
    seq_parts = lax.axis_size("seq")
    length = tokens * seq_parts
    query_width = queries.shape[2]
    head_count = query_width // HEAD_WIDTH
    key_groups = unrotated_key_rows.shape[2] // HEAD_WIDTH
    local_heads = head_count // seq_parts
    adapter_rank_size = adapter_down_weight.shape[1]
    share = max(1, seq_parts // key_groups)
    part_rows = tokens // share
    query_tokens = queries.reshape(rollout_count, tokens, head_count, HEAD_WIDTH)
    grad_tokens = attention_output_gradient.reshape(rollout_count, tokens, head_count, HEAD_WIDTH)
    key_arranged = arrange_rows(unrotated_key_rows, share, part_rows, key_groups)
    value_arranged = arrange_rows(value_projection_rows, share, part_rows, key_groups)
    query_heads, key_parted, value_parted, grad_heads = (
        lax.all_to_all(query_tokens, "seq", split_axis=2, concat_axis=1, tiled=True),
        lax.all_to_all(key_arranged, "seq", split_axis=2, concat_axis=1, tiled=True),
        lax.all_to_all(value_arranged, "seq", split_axis=2, concat_axis=1, tiled=True),
        lax.all_to_all(grad_tokens, "seq", split_axis=2, concat_axis=1, tiled=True),
    )
    paired = join_group(jnp.stack([key_parted, value_parted], axis=0), share, seq_parts, part_rows)
    key_heads = paired[0]
    value_heads = paired[1]
    local_keys = key_heads.shape[2]
    cosine, sine_table = rotary_tables(length, HEAD_WIDTH)
    positions = jnp.arange(length, dtype=jnp.int32)
    keep_mask = (positions[None, :] >= offsets[:, None]) & (positions[None, :] < lengths[:, None])
    grad_heads = jnp.where(keep_mask[:, :, None, None], grad_heads, jnp.zeros_like(grad_heads))
    rot_query = rotate(query_heads.astype(jnp.float32), cosine, sine_table, 1.0).astype(
        jnp.bfloat16
    )
    rot_key = rotate(key_heads.astype(jnp.float32), cosine, sine_table, 1.0).astype(jnp.bfloat16)
    block_rows = min(512, length)
    query_rolls = []
    key_rolls = []
    value_rolls = []
    for rollout_slot in range(rollout_count):
        query_list = []
        key_list = []
        value_list = []
        for head_slot in range(local_heads):
            key_slot = head_slot * local_keys // local_heads
            query_grad, key_grad, value_grad = head_backward(
                rot_query[rollout_slot, :, head_slot],
                rot_key[rollout_slot, :, key_slot],
                value_heads[rollout_slot, :, key_slot],
                grad_heads[rollout_slot, :, head_slot],
                offsets[rollout_slot],
                block_rows,
            )
            query_list.append(
                rotate(query_grad[:, None, :], cosine, sine_table, -1.0)[:, 0].astype(jnp.bfloat16)
            )
            key_list.append(
                rotate(key_grad[:, None, :], cosine, sine_table, -1.0)[:, 0].astype(jnp.bfloat16)
            )
            value_list.append(value_grad.astype(jnp.bfloat16))
        query_rolls.append(jnp.stack(query_list, axis=1))
        key_rolls.append(jnp.stack(key_list, axis=1))
        value_rolls.append(jnp.stack(value_list, axis=1))
    query_back = jnp.stack(query_rolls, axis=0)
    key_parts = jnp.stack(key_rolls, axis=0)
    value_parts = jnp.stack(value_rolls, axis=0)
    shared_heads = local_heads // local_keys
    key_local = (
        key_parts.astype(jnp.float32)
        .reshape(rollout_count, length, local_keys, shared_heads, HEAD_WIDTH)
        .sum(axis=3)
    )
    value_local = (
        value_parts.astype(jnp.float32)
        .reshape(rollout_count, length, local_keys, shared_heads, HEAD_WIDTH)
        .sum(axis=3)
    )
    summed = reduce_group(
        jnp.stack([key_local, value_local], axis=0), share, seq_parts, part_rows
    ).astype(jnp.bfloat16)
    query_result, key_result, value_result = (
        lax.all_to_all(query_back, "seq", split_axis=1, concat_axis=2, tiled=True),
        lax.all_to_all(summed[0], "seq", split_axis=1, concat_axis=2, tiled=True),
        lax.all_to_all(summed[1], "seq", split_axis=1, concat_axis=2, tiled=True),
    )
    key_total = jnp.transpose(
        key_result.reshape(rollout_count, part_rows, key_groups, share, HEAD_WIDTH), (0, 3, 1, 2, 4)
    ).reshape(rollout_count, tokens, key_groups * HEAD_WIDTH)
    value_total = jnp.transpose(
        value_result.reshape(rollout_count, part_rows, key_groups, share, HEAD_WIDTH),
        (0, 3, 1, 2, 4),
    ).reshape(rollout_count, tokens, key_groups * HEAD_WIDTH)
    flattened_query = query_result.reshape(rollout_count * tokens, query_width)
    hidden_state = normed_hidden_input.reshape(rollout_count * tokens, normed_hidden_input.shape[2])
    adapter_latent = jnp.dot(
        hidden_state, adapter_down_weight, preferred_element_type=jnp.float32
    ).astype(jnp.bfloat16)
    backward_gradient = contract_axes(flattened_query, adapter_up_weight, 1, 1).astype(jnp.bfloat16)
    joined_terms = lax.psum_scatter(
        jnp.concatenate(
            [
                contract_axes(hidden_state, backward_gradient, 0, 0),
                contract_axes(flattened_query, adapter_latent, 0, 0),
            ],
            axis=1,
        ).astype(jnp.bfloat16),
        "seq",
        scatter_dimension=0,
        tiled=True,
    ).astype(jnp.float32)
    down_local = joined_terms[:, :adapter_rank_size]
    up_local = joined_terms[:, adapter_rank_size:]
    down_sum, up_sum = (
        lax.psum(down_local.astype(jnp.bfloat16), "dp").astype(jnp.float32),
        lax.psum(up_local.astype(jnp.bfloat16), "dp").astype(jnp.float32),
    )
    return (
        flattened_query.reshape(rollout_count, tokens, query_width),
        key_total,
        value_total,
        down_sum,
        up_sum.T,
    )


VMEM_LIMIT = 48 * 1024 * 1024
NEG = -1e30
OFFSET_BOUND = 32


def nt_dot(left, right):
    return lax.dot_general(
        left, right, (((1,), (1,)), ((), ())), preferred_element_type=jnp.float32
    )


def fused_kernel(
    n_seq,
    n_dp,
    n_roll,
    tokens,
    kv_heads,
    group,
    rank,
    off_hbm,
    len_hbm,
    cos_hbm,
    sin_hbm,
    q_hbm,
    k_hbm,
    v_hbm,
    g_hbm,
    hid_hbm,
    down_hbm,
    up_hbm,
    gq_ref,
    gk_ref,
    gv_ref,
    gd_ref,
    gu_ref,
    off_ref,
    len_ref,
    cos_ref,
    sin_ref,
    k_raw,
    kv_own,
    kv_all,
    q_all,
    g_all,
    hid_own,
    hid_other,
    down_ref,
    up_ref,
    lat_all,
    lat_roll,
    score_buf,
    prob_buf,
    dkv_own,
    dkv_all,
    gq_all,
    back_acc,
    back_got,
    up_acc,
    up_own,
    up_got,
    dn_own,
    dn_got,
    z_own,
    z_got,
    z_all,
    loc_sem,
    v_sem,
    ql_sem,
    gl_sem,
    kv_send,
    kv_recv,
    q_send,
    q_recv,
    g_send,
    g_recv,
    hid_send,
    hid_recv,
    one_send,
    one_recv,
    dk_send,
    dk_recv,
    gq_send,
    gq_recv,
    ad_send,
    ad_recv,
    rs_send,
    rs_recv,
    ag_send,
    ag_recv,
):
    me = lax.axis_index("seq")
    my_dp = lax.axis_index("dp")
    chip = me // 2
    core = me % 2
    partner = me + 1 - 2 * core
    n_chips = n_seq // 2
    n_own = kv_heads // 2
    width = HEAD_WIDTH
    half = width // 2
    span = group * width
    chip_tokens = 2 * tokens
    rows = group * chip_tokens
    scale = width ** (-0.5)
    exp_scale = scale * math.log2(math.e)
    piece = span // n_dp

    def lanes(index, size):
        return pl.ds(pl.multiple_of(index * size, size), size)

    def seq_rows(device):
        return pl.ds(pl.multiple_of(device * tokens, tokens), tokens)

    def local(src, dst, sem):
        return pltpu.make_async_copy(src, dst, sem)

    def remote(src, dst, send, recv, where):
        return pltpu.make_async_remote_copy(
            src_ref=src, dst_ref=dst, send_sem=send, recv_sem=recv, device_id=where
        )

    def each_unit(body):
        def step(index, carry):
            body(index // n_roll, index % n_roll)
            return carry

        lax.fori_loop(0, n_own * n_roll, step, 0)

    barrier = pltpu.get_barrier_semaphore()
    for step in range(1, n_seq):
        pl.semaphore_signal(barrier, inc=1, device_id={"seq": lax.rem(me + step, n_seq)})
    for step in range(1, n_dp):
        pl.semaphore_signal(barrier, inc=1, device_id={"dp": lax.rem(my_dp + step, n_dp)})

    chip_rows = pl.ds(pl.multiple_of(chip * chip_tokens, chip_tokens), chip_tokens)
    k_load = local(k_hbm, k_raw, loc_sem.at[0])
    cos_load = local(cos_hbm.at[chip_rows], cos_ref, loc_sem.at[1])
    sin_load = local(sin_hbm.at[chip_rows], sin_ref, loc_sem.at[2])
    off_load = local(off_hbm, off_ref, loc_sem.at[3])
    len_load = local(len_hbm, len_ref, loc_sem.at[4])
    hid_load = local(hid_hbm, hid_own, loc_sem.at[5])
    down_load = local(down_hbm, down_ref, loc_sem.at[6])
    up_load = local(up_hbm, up_ref, loc_sem.at[7])

    def v_load(h):
        return local(v_hbm.at[:, :, lanes(h, width)], kv_own.at[h, :, 1], v_sem.at[h])

    def q_load(i, r):
        h = 2 * i + core
        return local(q_hbm.at[r, :, lanes(h, span)], q_all.at[i, r, core], ql_sem.at[i, r])

    def g_load(i, r):
        h = 2 * i + core
        return local(g_hbm.at[r, :, lanes(h, span)], g_all.at[i, r, core], gl_sem.at[i, r])

    def load_queries(i, r):
        q_load(i, r).start()
        g_load(i, r).start()

    k_load.start()
    cos_load.start()
    sin_load.start()
    for h in range(kv_heads):
        v_load(h).start()
    off_load.start()
    len_load.start()
    each_unit(load_queries)
    hid_load.start()
    down_load.start()
    up_load.start()

    def q_copy(i, r):
        h = 2 * i + 1 - core
        return remote(
            q_hbm.at[r, :, lanes(h, span)],
            q_all.at[i, r, core],
            q_send.at[i, r],
            q_recv.at[i, r],
            {"seq": partner},
        )

    def g_copy(i, r):
        h = 2 * i + 1 - core
        return remote(
            g_hbm.at[r, :, lanes(h, span)],
            g_all.at[i, r, core],
            g_send.at[i, r],
            g_recv.at[i, r],
            {"seq": partner},
        )

    def hid_copy(i):
        h = 2 * i + 1 - core
        return remote(
            hid_hbm.at[:, :, lanes(h, span)],
            hid_other.at[i],
            hid_send.at[i],
            hid_recv.at[i],
            {"seq": partner},
        )

    def send_queries(i, r):
        q_copy(i, r).start()
        g_copy(i, r).start()

    def gather_copy(i, r, parity, chip_step):
        h = 2 * i + parity
        return remote(
            kv_own.at[h, r],
            kv_all.at[i, r, :, seq_rows(me), :],
            kv_send.at[i, r, parity, chip_step],
            kv_recv.at[i, r, me],
            {"seq": 2 * (chip + chip_step) + parity},
        )

    def pair_copy(i, r):
        h = 2 * i + 1 - core
        return remote(
            kv_own.at[h, r],
            kv_all.at[i, r, :, seq_rows(me), :],
            kv_send.at[i, r, 0, 0],
            kv_recv.at[i, r, me],
            {"seq": partner},
        )

    def gather_ops(i, r, act):
        act(pair_copy(i, r))
        for chip_step in range(1, n_chips):

            @pl.when(chip + chip_step < n_chips)
            def _():
                for parity in range(2):
                    act(gather_copy(i, r, parity, chip_step))

    def gather_wait(i, r):
        def got(device):
            remote(
                kv_own.at[0, r],
                kv_all.at[i, r, :, seq_rows(device), :],
                kv_send.at[i, r, 0, 0],
                kv_recv.at[i, r, device],
                {"seq": partner},
            ).wait_recv()

        got(partner)
        for source in range(n_chips - 1):

            @pl.when(source < chip)
            def _():
                got(2 * source)
                got(2 * source + 1)

    def reduce_copy(i, r, target_chip, target_core):
        target = 2 * target_chip + target_core
        return remote(
            dkv_own.at[i, r, :, seq_rows(target), :],
            dkv_all.at[chip, 2 * i + core, r],
            dk_send.at[i, r, target_chip, target_core],
            dk_recv.at[chip, 2 * i + core, r],
            {"seq": target},
        )

    def reduce_ops(i, r, act):
        for target_chip in range(n_chips - 1):

            @pl.when(target_chip < chip)
            def _():
                for target_core in range(2):
                    act(reduce_copy(i, r, target_chip, target_core))

        act(reduce_copy(i, r, chip, 1 - core))

    def reduce_got(source, h, r):
        return remote(
            dkv_own.at[0, 0, :, pl.ds(0, tokens), :],
            dkv_all.at[source, h, r],
            dk_send.at[0, 0, 0, 0],
            dk_recv.at[source, h, r],
            {"seq": partner},
        )

    def gq_copy(i, r, parity):
        return remote(
            gq_all.at[i, r, 1 - core],
            gq_ref.at[r, :, lanes(2 * i + parity, span)],
            gq_send.at[i, r],
            gq_recv.at[i, r],
            {"seq": partner},
        )

    def adapter_copy(t, own, got, source, target_chip):
        return remote(
            own.at[target_chip],
            got.at[source],
            ad_send.at[t, target_chip],
            ad_recv.at[t, source],
            {"seq": 2 * target_chip + core},
        )

    pl.semaphore_wait(barrier, n_seq + n_dp - 2)

    k_load.wait()
    cos_load.wait()
    sin_load.wait()
    own_rows = pl.ds(pl.multiple_of(core * tokens, tokens), tokens)
    cos_own = cos_ref[own_rows, :]
    sin_own = sin_ref[own_rows, :]
    for h in range(kv_heads):
        for r in range(n_roll):
            key = k_raw[r, :, h * width : (h + 1) * width].astype(jnp.float32)
            key = key * cos_own + pltpu.roll(key, half, 1) * sin_own
            kv_own[h, r, 0] = key.astype(jnp.bfloat16)
    for h in range(kv_heads):
        v_load(h).wait()
    each_unit(lambda i, r: gather_ops(i, r, lambda copy: copy.start()))
    each_unit(send_queries)

    for i in range(n_own):
        for r in range(n_roll):
            kv_all[i, r, :, seq_rows(me), :] = kv_own[2 * i + core, r]

    hid_load.wait()
    down_load.wait()
    flat = n_roll * tokens
    hid_rows = hid_own[...].reshape(flat, hid_own.shape[2])
    lat_all[core] = nt_dot(down_ref[...], hid_rows).astype(jnp.bfloat16)
    lat_copy = remote(
        lat_all.at[core], lat_all.at[core], one_send.at[0], one_recv.at[0], {"seq": partner}
    )
    lat_copy.start()
    for i in range(n_own):
        hid_copy(i).start()
    back_acc[...] = jnp.zeros_like(back_acc)
    up_acc[...] = jnp.zeros_like(up_acc)
    up_load.wait()
    off_load.wait()
    len_load.wait()
    remote(
        lat_all.at[core], lat_all.at[1 - core], one_send.at[0], one_recv.at[0], {"seq": partner}
    ).wait_recv()
    for r in range(n_roll):
        lane = slice(r * tokens, (r + 1) * tokens)
        lat_roll[r] = jnp.concatenate([lat_all[0, :, lane], lat_all[1, :, lane]], axis=1)

    def attend(i, r, blocks):
        n_keys = blocks * chip_tokens
        offset = off_ref[r]
        position = chip * chip_tokens + lax.broadcasted_iota(jnp.int32, (chip_tokens, width), 0)
        keep = (position >= offset) & (position < len_ref[r])
        cos = cos_ref[...]
        sin = sin_ref[...]
        queries = []
        grads = []
        for j in range(group):
            lane = slice(j * width, (j + 1) * width)
            query = q_all[i, r, :, :, lane].reshape(chip_tokens, width).astype(jnp.float32)
            query = query * cos + pltpu.roll(query, half, 1) * sin
            queries.append(query.astype(jnp.bfloat16))
            grad = g_all[i, r, :, :, lane].reshape(chip_tokens, width).astype(jnp.float32)
            grads.append(jnp.where(keep, grad, 0.0).astype(jnp.bfloat16))
        query = jnp.concatenate(queries, axis=0)
        grad = jnp.concatenate(grads, axis=0)
        key = kv_all[i, r, 0, :n_keys, :]

        row_max = None
        for b in range(blocks):
            keys = slice(b * chip_tokens, (b + 1) * chip_tokens)
            score = nt_dot(kv_all[i, r, 0, keys, :], query)
            if b == blocks - 1 or b * chip_tokens < OFFSET_BOUND:
                key_row = lax.broadcasted_iota(jnp.int32, (chip_tokens, rows), 0)
                visible = key_row + b * chip_tokens >= offset
                if b == blocks - 1:
                    query_row = lax.broadcasted_iota(jnp.int32, (chip_tokens, rows), 1) % chip_tokens
                    visible = (key_row == query_row) | (visible & (key_row <= query_row))
                score = jnp.where(visible, score, NEG)
            score_buf[0, keys, :] = score
            part = jnp.max(score, axis=0, keepdims=True)
            row_max = part if row_max is None else jnp.maximum(row_max, part)
        total = None
        delta = None
        for b in range(blocks):
            keys = slice(b * chip_tokens, (b + 1) * chip_tokens)
            weight = jnp.exp2((score_buf[0, keys, :] - row_max) * exp_scale)
            grad_prob = nt_dot(kv_all[i, r, 1, keys, :], grad)
            score_buf[0, keys, :] = weight
            score_buf[1, keys, :] = grad_prob
            part = jnp.sum(weight, axis=0, keepdims=True)
            total = part if total is None else total + part
            part = jnp.sum(weight * grad_prob, axis=0, keepdims=True)
            delta = part if delta is None else delta + part
        inverse = 1.0 / total
        delta = delta * inverse
        inverse_scaled = inverse * scale
        for b in range(blocks):
            keys = slice(b * chip_tokens, (b + 1) * chip_tokens)
            weight = score_buf[0, keys, :]
            prob = (weight * inverse).astype(jnp.bfloat16)
            slope = ((weight * inverse_scaled) * (score_buf[1, keys, :] - delta)).astype(jnp.bfloat16)
            prob_buf[keys, :] = slope
            dkv_own[i, r, 1, keys, :] = jnp.dot(
                prob, grad, preferred_element_type=jnp.float32
            ).astype(jnp.bfloat16)
            dkv_own[i, r, 0, keys, :] = jnp.dot(
                slope, query, preferred_element_type=jnp.float32
            ).astype(jnp.bfloat16)
        back = jnp.dot(key.T, prob_buf[:n_keys, :], preferred_element_type=jnp.float32).T
        for j in range(group):
            part = back[j * chip_tokens : (j + 1) * chip_tokens]
            part = part * cos - pltpu.roll(part, half, 1) * sin
            part = part.astype(jnp.bfloat16).reshape(2, tokens, width)
            gq_all[i, r, :, :, j * width : (j + 1) * width] = part

    def unit(i, r):
        h = 2 * i + core
        gather_wait(i, r)
        q_load(i, r).wait()
        g_load(i, r).wait()
        remote(
            q_hbm.at[r, :, lanes(h, span)],
            q_all.at[i, r, 1 - core],
            q_send.at[i, r],
            q_recv.at[i, r],
            {"seq": partner},
        ).wait_recv()
        remote(
            g_hbm.at[r, :, lanes(h, span)],
            g_all.at[i, r, 1 - core],
            g_send.at[i, r],
            g_recv.at[i, r],
            {"seq": partner},
        ).wait_recv()
        for blocks in range(1, n_chips + 1):

            @pl.when(chip == blocks - 1)
            def _():
                attend(i, r, blocks)

        reduce_ops(i, r, lambda copy: copy.start())
        gq_copy(i, r, core).start()
        dkv_all[chip, h, r] = dkv_own[i, r, :, seq_rows(me), :]
        gq_ref[r, :, lanes(h, span)] = gq_all[i, r, core]
        grad_query = gq_all[i, r].reshape(chip_tokens, span)
        back_acc[r] = back_acc[r] + nt_dot(up_ref[:, lanes(h, span)], grad_query)
        up_part = jnp.dot(lat_roll[r], grad_query, preferred_element_type=jnp.float32)
        up_total = jnp.where(r == 0, 0.0, up_acc[...]) + up_part
        up_acc[...] = up_total

        @pl.when(r == n_roll - 1)
        def _():
            up_own[i] = up_total.astype(jnp.bfloat16)

            @pl.when(i != chip)
            def _():
                adapter_copy(1, up_own, up_got, chip, i).start()

    each_unit(unit)

    back_copy = remote(back_acc, back_got, one_send.at[1], one_recv.at[1], {"seq": partner})
    back_copy.start()
    for i in range(n_own):
        hid_copy(i).wait_recv()
    back_copy.wait_recv()
    sums = [(back_acc[r] + back_got[r]).astype(jnp.bfloat16) for r in range(n_roll)]
    first = jnp.concatenate([part[:, :tokens] for part in sums], axis=1)
    second = jnp.concatenate([part[:, tokens:] for part in sums], axis=1)
    back_own = jnp.where(core == 0, first, second)
    back_other = jnp.where(core == 0, second, first)
    for i in range(n_own):
        own = hid_own[:, :, lanes(2 * i + core, span)].reshape(flat, span)
        other = hid_other[i].reshape(flat, span)
        dn_own[i] = (
            jnp.dot(back_own, own, preferred_element_type=jnp.float32)
            + jnp.dot(back_other, other, preferred_element_type=jnp.float32)
        ).astype(jnp.bfloat16)

        @pl.when(i != chip)
        def _():
            adapter_copy(0, dn_own, dn_got, chip, i).start()

    def owner_sum(t, own, got):
        total = own[chip].astype(jnp.float32)
        for step in range(1, n_chips):
            source = lax.rem(chip + step, n_chips)
            adapter_copy(t, own, got, source, 0).wait_recv()
            total = total + got[source].astype(jnp.float32)
        z_own[t] = total.astype(jnp.bfloat16)

    def scatter_copy(t, target):
        return remote(
            z_own.at[t, :, lanes(target, piece)],
            z_got.at[t, my_dp],
            rs_send.at[t, target],
            rs_recv.at[t, my_dp],
            {"dp": target},
        )

    def scatter_start(t):
        for step in range(1, n_dp):
            scatter_copy(t, lax.rem(my_dp + step, n_dp)).start()

    def collect_copy(t, target):
        return remote(
            z_all.at[t, my_dp],
            z_all.at[t, my_dp],
            ag_send.at[t, target],
            ag_recv.at[t, my_dp],
            {"dp": target},
        )

    def collect_start(t):
        total = z_own[t, :, lanes(my_dp, piece)].astype(jnp.float32)
        for step in range(1, n_dp):
            source = lax.rem(my_dp + step, n_dp)
            remote(
                z_own.at[t, :, lanes(source, piece)],
                z_got.at[t, source],
                rs_send.at[t, source],
                rs_recv.at[t, source],
                {"dp": source},
            ).wait_recv()
            total = total + z_got[t, source].astype(jnp.float32)
        z_all[t, my_dp] = total.astype(jnp.bfloat16)
        for step in range(1, n_dp):
            collect_copy(t, lax.rem(my_dp + step, n_dp)).start()

    def collect_out(t, out):
        for step in range(1, n_dp):
            source = lax.rem(my_dp + step, n_dp)
            remote(
                z_all.at[t, source],
                z_all.at[t, source],
                ag_send.at[t, source],
                ag_recv.at[t, source],
                {"dp": source},
            ).wait_recv()
        for d in range(n_dp):
            out[:, d * piece : (d + 1) * piece] = z_all[t, d].astype(jnp.float32)

    owner_sum(1, up_own, up_got)
    scatter_start(1)

    cos_own = cos_ref[own_rows, :]
    sin_own = sin_ref[own_rows, :]

    def finish(h, r):
        @pl.when(h % 2 != core)
        def _():
            reduce_got(chip, h, r).wait_recv()

        for source in range(1, n_chips):

            @pl.when(source > chip)
            def _():
                reduce_got(source, h, r).wait_recv()

        def add(source, totals):
            return tuple(
                totals[t] + dkv_all[source, h, r, t].astype(jnp.float32) for t in range(2)
            )

        first = tuple(dkv_all[chip, h, r, t].astype(jnp.float32) for t in range(2))
        key, value = lax.fori_loop(chip + 1, n_chips, add, first)
        key = key * cos_own - pltpu.roll(key, half, 1) * sin_own
        gk_ref[r, :, lanes(h, width)] = key.astype(jnp.bfloat16)
        gv_ref[r, :, lanes(h, width)] = value.astype(jnp.bfloat16)

    def finish_step(index, carry):
        finish(index // n_roll, index % n_roll)
        return carry

    lax.fori_loop(0, kv_heads * n_roll, finish_step, 0)

    collect_start(1)
    owner_sum(0, dn_own, dn_got)
    scatter_start(0)
    collect_out(1, gu_ref)
    each_unit(lambda i, r: gq_copy(i, r, 1 - core).wait_recv())
    collect_start(0)

    each_unit(lambda i, r: gather_ops(i, r, lambda copy: copy.wait_send()))
    each_unit(lambda i, r: reduce_ops(i, r, lambda copy: copy.wait_send()))

    def sent(i, r):
        q_copy(i, r).wait_send()
        g_copy(i, r).wait_send()
        gq_copy(i, r, core).wait_send()

    each_unit(sent)
    lat_copy.wait_send()
    back_copy.wait_send()
    for i in range(n_own):
        hid_copy(i).wait_send()

        @pl.when(i != chip)
        def _():
            adapter_copy(0, dn_own, dn_got, chip, i).wait_send()
            adapter_copy(1, up_own, up_got, chip, i).wait_send()

    collect_out(0, gd_ref)
    for t in range(2):
        for step in range(1, n_dp):
            target = lax.rem(my_dp + step, n_dp)
            scatter_copy(t, target).wait_send()
            collect_copy(t, target).wait_send()


def write_kernel(n_outs, *refs):
    sem = refs[2 * n_outs]
    copies = [
        pltpu.make_async_copy(refs[n], refs[n_outs + n], sem.at[n]) for n in range(n_outs)
    ]
    for copy in copies:
        copy.start()
    for copy in copies:
        copy.wait()


def fused_on_device(
    n_seq,
    n_dp,
    queries,
    unrotated_key_rows,
    value_projection_rows,
    attention_output_gradient,
    normed_hidden_input,
    adapter_down_weight,
    adapter_up_weight,
    lengths,
    offsets,
):
    n_roll, tokens, q_width = queries.shape
    kv_width = unrotated_key_rows.shape[2]
    kv_heads = kv_width // HEAD_WIDTH
    group = q_width // kv_width
    rank = adapter_down_weight.shape[1]
    length = n_seq * tokens
    n_chips = n_seq // 2
    n_own = kv_heads // 2
    half = HEAD_WIDTH // 2
    frequency = rotary_base ** (-(np.arange(half, dtype=np.float32) * 2.0 / HEAD_WIDTH))
    angles = np.arange(length, dtype=np.float32)[:, None] * frequency.astype(np.float32)[None, :]
    cosine, sine = np.cos(angles), np.sin(angles)
    cos_wide = np.concatenate([cosine, cosine], axis=1).astype(np.float32)
    sin_wide = np.concatenate([-sine, sine], axis=1).astype(np.float32)
    span = q_width // n_seq
    low = jnp.bfloat16
    full = jnp.float32
    dma = pltpu.SemaphoreType.DMA
    vm = pltpu.VMEM
    anywhere = pl.BlockSpec(memory_space=pl.ANY)
    vmem = pl.BlockSpec(memory_space=pltpu.VMEM)
    out_types = [
        ((n_roll, tokens, q_width), low),
        ((n_roll, tokens, kv_width), low),
        ((n_roll, tokens, kv_width), low),
        ((rank, span), full),
        ((rank, span), full),
    ]
    outs = pl.pallas_call(
        partial(fused_kernel, n_seq, n_dp, n_roll, tokens, kv_heads, group, rank),
        out_shape=[vm(shape, kind) for shape, kind in out_types],
        in_specs=[anywhere] * 11,
        out_specs=[vmem] * len(out_types),
        scratch_shapes=[
            pltpu.SMEM((n_roll,), jnp.int32),
            pltpu.SMEM((n_roll,), jnp.int32),
            vm((2 * tokens, HEAD_WIDTH), full),
            vm((2 * tokens, HEAD_WIDTH), full),
            vm((n_roll, tokens, kv_width), low),
            vm((kv_heads, n_roll, 2, tokens, HEAD_WIDTH), low),
            vm((n_own, n_roll, 2, length, HEAD_WIDTH), low),
            vm((n_own, n_roll, 2, tokens, span), low),
            vm((n_own, n_roll, 2, tokens, span), low),
            vm((n_roll, tokens, q_width), low),
            vm((n_own, n_roll, tokens, span), low),
            vm((rank, q_width), low),
            vm((rank, q_width), low),
            vm((2, rank, n_roll * tokens), low),
            vm((n_roll, rank, 2 * tokens), low),
            vm((2, length, group * 2 * tokens), full),
            vm((length, group * 2 * tokens), low),
            vm((n_own, n_roll, 2, length, HEAD_WIDTH), low),
            vm((n_chips, kv_heads, n_roll, 2, tokens, HEAD_WIDTH), low),
            vm((n_own, n_roll, 2, tokens, span), low),
            vm((n_roll, rank, 2 * tokens), full),
            vm((n_roll, rank, 2 * tokens), full),
            vm((rank, span), full),
            vm((n_own, rank, span), low),
            vm((n_chips, rank, span), low),
            vm((n_own, rank, span), low),
            vm((n_chips, rank, span), low),
            vm((2, rank, span), low),
            vm((2, n_dp, rank, span // n_dp), low),
            vm((2, n_dp, rank, span // n_dp), low),
            dma((8,)),
            dma((kv_heads,)),
            dma((n_own, n_roll)),
            dma((n_own, n_roll)),
            dma((n_own, n_roll, 2, n_chips)),
            dma((n_own, n_roll, n_seq)),
            dma((n_own, n_roll)),
            dma((n_own, n_roll)),
            dma((n_own, n_roll)),
            dma((n_own, n_roll)),
            dma((n_own,)),
            dma((n_own,)),
            dma((2,)),
            dma((2,)),
            dma((n_own, n_roll, n_chips, 2)),
            dma((n_chips, kv_heads, n_roll)),
            dma((n_own, n_roll)),
            dma((n_own, n_roll)),
            dma((2, n_chips)),
            dma((2, n_chips)),
            dma((2, n_dp)),
            dma((2, n_dp)),
            dma((2, n_dp)),
            dma((2, n_dp)),
        ],
        compiler_params=pltpu.CompilerParams(
            collective_id=0, has_side_effects=True, vmem_limit_bytes=VMEM_LIMIT
        ),
    )(
        offsets,
        lengths,
        jnp.asarray(cos_wide),
        jnp.asarray(sin_wide),
        queries,
        unrotated_key_rows,
        value_projection_rows,
        attention_output_gradient,
        normed_hidden_input,
        adapter_down_weight.T,
        adapter_up_weight,
    )
    outs = pl.pallas_call(
        partial(write_kernel, len(out_types)),
        out_shape=[jax.ShapeDtypeStruct(shape, kind) for shape, kind in out_types],
        in_specs=[vmem] * len(out_types),
        out_specs=[anywhere] * len(out_types),
        scratch_shapes=[dma((len(out_types),))],
        compiler_params=pltpu.CompilerParams(vmem_limit_bytes=8 * 1024 * 1024),
    )(*outs)
    grad_query, grad_key, grad_value, grad_down, grad_up = outs
    return (grad_query, grad_key, grad_value, grad_down.T, grad_up)


def dispatch(mesh, *args):
    n_seq = mesh.shape["seq"]
    n_dp = mesh.shape["dp"]
    n_roll, tokens, q_width = args[0].shape
    kv_width = args[1].shape[2]
    kv_heads = kv_width // HEAD_WIDTH
    group = q_width // kv_width
    rows = 2 * tokens * group
    length = n_seq * tokens
    held = 3 * 2 * n_roll * length * kv_width + 10 * n_roll * tokens * q_width
    held = held + 12 * length * rows
    fits = held < VMEM_LIMIT // 2
    whole = kv_heads == n_seq and n_seq % 2 == 0 and 2 * tokens == HEAD_WIDTH
    whole = whole and 2 * tokens >= OFFSET_BOUND and (group * HEAD_WIDTH) % (n_dp * 128) == 0
    if not (fits and whole):
        return on_device(*args)
    return fused_on_device(n_seq, n_dp, *args)


def solution(mesh):
    in_specs = (
        P("dp", "seq", None),
        P("dp", "seq", None),
        P("dp", "seq", None),
        P("dp", "seq", None),
        P("dp", "seq", None),
        P(),
        P(),
        P("dp"),
        P("dp"),
    )
    out_specs = (
        P("dp", "seq", None),
        P("dp", "seq", None),
        P("dp", "seq", None),
        P("seq", None),
        P(None, "seq"),
    )
    return jax.shard_map(
        partial(dispatch, mesh), mesh=mesh, in_specs=in_specs, out_specs=out_specs, check_vma=False
    )
```

time: 81.7 us -> 68.4 us (0.84)
  Pallas kernels: 73.9 us -> 58.3 us
  local copies, waits for them, and re-layouts: 5.98 us -> 8.98 us
  other arithmetic: 0.93 us -> 0 us
    pallas_call x1, Pallas kernels: 73.9 us -> 57 us  [fused_on_device(): pl.pallas_call(partial(fused_kernel, n_seq, n_dp, n_roll, tokens, kv_head...]
    unnamed x13 -> x20, local copies, waits for them, and re-layouts: 5.98 us -> 8.98 us
    pallas_call x0 -> x1, Pallas kernels: none -> 1.26 us  [fused_on_device(): pl.pallas_call(partial(write_kernel, len(out_types)), out_shape=[jax.Shap...]
where the time goes in v1:
time: 68.4 us; the launch traced here: 67.9 us
  Pallas kernels  58.3 us (85%)
  local copies, waits for them, and re-layouts  8.98 us (13%)
    pallas_call x1, Pallas kernels, fused_on_device(): pl.pallas_call(partial(fused_kernel, n_seq, n_dp, n_roll, tokens, kv_head...  57 us
    unnamed x20, local copies, waits for them, and re-layouts  8.98 us

profile of v1, /device:TPU:0, one launch (start us, length us, event | category | flops | bytes accessed | tf_op | source)
XLA Modules:
  0.0 67.9 jit_solution(11309614109591616954)
XLA Ops:
  0.6 0.0 copy-start.8
  0.6 0.0 copy-start.9
  0.7 0.6 copy-done.8
  1.3 0.0 copy-done.9
  1.3 0.0 copy-start
  1.3 1.2 %copy-done = bf16[2,64,4096]{2,1,0:T(8,128)(2,1)S(1)} copy-done((bf16[2,64,4096]{2,1,0:T(8,128)(2,1)S(1)}, bf16[2,64,4096]{2,1,0:T(8,128)(2,1)}, u32[]{:S(2)}) %copy-start) | copy-done | bytes 1048600
  2.5 0.0 copy-start.1
  2.5 1.2 %copy-done.1 = bf16[2,64,4096]{2,1,0:T(8,128)(2,1)S(1)} copy-done((bf16[2,64,4096]{2,1,0:T(8,128)(2,1)S(1)}, bf16[2,64,4096]{2,1,0:T(8,128)(2,1)}, u32[]{:S(2)}) %copy-start.1) | copy-done | bytes 1048600
  3.8 0.0 copy-start.2
  3.8 1.0 %copy-done.2 = bf16[4096,64]{0,1:T(8,128)(2,1)S(1)} copy-done((bf16[4096,64]{0,1:T(8,128)(2,1)S(1)}, bf16[4096,64]{0,1:T(8,128)(2,1)}, u32[]{:S(2)}) %copy-start.2) | copy-done | bytes 524312
  4.8 0.0 copy-start.3
  4.8 1.0 %copy-done.3 = bf16[64,4096]{1,0:T(8,128)(2,1)S(1)} copy-done((bf16[64,4096]{1,0:T(8,128)(2,1)S(1)}, bf16[64,4096]{1,0:T(8,128)(2,1)}, u32[]{:S(2)}) %copy-start.3) | copy-done | bytes 524312
  5.8 0.0 copy-start.4
  5.8 0.9 %copy-done.4 = bf16[2,64,1024]{2,1,0:T(8,128)(2,1)S(1)} copy-done((bf16[2,64,1024]{2,1,0:T(8,128)(2,1)S(1)}, bf16[2,64,1024]{2,1,0:T(8,128)(2,1)}, u32[]{:S(2)}) %copy-start.4) | copy-done | bytes 262168
  6.8 0.0 copy-start.5
  6.8 0.9 %copy-done.5 = bf16[2,64,1024]{2,1,0:T(8,128)(2,1)S(1)} copy-done((bf16[2,64,1024]{2,1,0:T(8,128)(2,1)S(1)}, bf16[2,64,1024]{2,1,0:T(8,128)(2,1)}, u32[]{:S(2)}) %copy-start.5) | copy-done | bytes 262168
  7.7 0.0 copy-start.6
  7.7 0.9 %copy-done.6 = f32[512,128]{1,0:T(8,128)S(1)} copy-done((f32[512,128]{1,0:T(8,128)S(1)}, f32[512,128]{1,0:T(8,128)}, u32[]{:S(2)}) %copy-start.6) | copy-done | bytes 262168
  8.7 0.0 copy-start.7
  8.7 0.9 %copy-done.7 = f32[512,128]{1,0:T(8,128)S(1)} copy-done((f32[512,128]{1,0:T(8,128)S(1)}, f32[512,128]{1,0:T(8,128)}, u32[]{:S(2)}) %copy-start.7) | copy-done | bytes 262168
  9.6 57.0 %shard_map.146 = (bf16[2,64,4096]{2,1,0:T(8,128)(2,1)S(1)}, bf16[2,64,1024]{2,1,0:T(8,128)(2,1)S(1)}, bf16[2,64,1024]{2,1,0:T(8,128)(2,1)S(1)}, f32[64,512]{1,0:T(8,128)S(1)}, f32[64,512]{1,0:T(8,128)S(1)}) custom-call(s32[2]{0:T(128)S(1)} %copy-done.8, s32[2]{0:T(128)S(1)} %copy-done.9, f32[512,128]{1,0:T(8,128)S(1)} %copy-done.7, ...), custom_call_target="tpu_custom_call" | custom-call | tf_op jit(solution)/shard_map/pallas_call | solution.py:948
  66.7 1.3 %shard_map.147 = (bf16[2,64,4096]{2,1,0:T(8,128)(2,1)}, bf16[2,64,1024]{2,1,0:T(8,128)(2,1)}, bf16[2,64,1024]{2,1,0:T(8,128)(2,1)}, f32[64,512]{1,0:T(8,128)}, f32[64,512]{1,0:T(8,128)}) custom-call(bf16[2,64,4096]{2,1,0:T(8,128)(2,1)S(1)} %get-tuple-element.15.refs_0_, bf16[2,64,1024]{2,1,0:T(8,128)(2,1)S(1)} %get-tuple-element.16.refs_1_, ...), custom_call_target="tpu_custom_call" | custom-call | tf_op jit(solution)/shard_map/pallas_call | solution.py:1025
Async XLA Ops:
  0.6 0.7 copy-start.8
  0.6 0.7 copy-start.9
  1.3 1.2 %copy-start = (bf16[2,64,4096]{2,1,0:T(8,128)(2,1)S(1)}, bf16[2,64,4096]{2,1,0:T(8,128)(2,1)}, u32[]{:S(2)}) copy-start(bf16[2,64,4096]{2,1,0:T(8,128)(2,1)} %q_hbm.1) | copy-start | bytes 3145732
  2.5 1.2 %copy-start.1 = (bf16[2,64,4096]{2,1,0:T(8,128)(2,1)S(1)}, bf16[2,64,4096]{2,1,0:T(8,128)(2,1)}, u32[]{:S(2)}) copy-start(bf16[2,64,4096]{2,1,0:T(8,128)(2,1)} %g_hbm.1) | copy-start | bytes 3145732
  3.8 1.0 %copy-start.2 = (bf16[4096,64]{0,1:T(8,128)(2,1)S(1)}, bf16[4096,64]{0,1:T(8,128)(2,1)}, u32[]{:S(2)}) copy-start(bf16[4096,64]{0,1:T(8,128)(2,1)} %param.16) | copy-start | bytes 1572868
  4.8 1.0 %copy-start.3 = (bf16[64,4096]{1,0:T(8,128)(2,1)S(1)}, bf16[64,4096]{1,0:T(8,128)(2,1)}, u32[]{:S(2)}) copy-start(bf16[64,4096]{1,0:T(8,128)(2,1)} %up_hbm.1) | copy-start | bytes 1572868
  5.8 0.9 %copy-start.4 = (bf16[2,64,1024]{2,1,0:T(8,128)(2,1)S(1)}, bf16[2,64,1024]{2,1,0:T(8,128)(2,1)}, u32[]{:S(2)}) copy-start(bf16[2,64,1024]{2,1,0:T(8,128)(2,1)} %k_hbm.1) | copy-start | bytes 786436
  6.8 0.9 %copy-start.5 = (bf16[2,64,1024]{2,1,0:T(8,128)(2,1)S(1)}, bf16[2,64,1024]{2,1,0:T(8,128)(2,1)}, u32[]{:S(2)}) copy-start(bf16[2,64,1024]{2,1,0:T(8,128)(2,1)} %v_hbm.1) | copy-start | bytes 786436
  7.7 0.9 %copy-start.6 = (f32[512,128]{1,0:T(8,128)S(1)}, f32[512,128]{1,0:T(8,128)}, u32[]{:S(2)}) copy-start(f32[512,128]{1,0:T(8,128)} %constant.5.clone.sin_hbm) | copy-start | bytes 786436
  8.7 0.9 %copy-start.7 = (f32[512,128]{1,0:T(8,128)S(1)}, f32[512,128]{1,0:T(8,128)}, u32[]{:S(2)}) copy-start(f32[512,128]{1,0:T(8,128)} %constant.4.clone.cos_hbm) | copy-start | bytes 786436

commit v2 on v1

--- a/solution.py
+++ b/solution.py
@@ -289,6 +289,9 @@
 
 
 VMEM_LIMIT = 48 * 1024 * 1024
+MERGE_LAG = 3
+HELD = 3
+SEND_AHEAD = 2
 NEG = -1e30
 OFFSET_BOUND = 32
 
@@ -353,6 +356,8 @@
     z_own,
     z_got,
     z_all,
+    merge_buf,
+    relay_buf,
     loc_sem,
     v_sem,
     ql_sem,
@@ -377,6 +382,11 @@
     rs_recv,
     ag_send,
     ag_recv,
+    fw_send,
+    mg_send,
+    mg_recv,
+    rl_send,
+    rl_recv,
 ):
     me = lax.axis_index("seq")
     my_dp = lax.axis_index("dp")
@@ -393,6 +403,7 @@
     scale = width ** (-0.5)
     exp_scale = scale * math.log2(math.e)
     piece = span // n_dp
+    n_units = n_own * n_roll
 
     def lanes(index, size):
         return pl.ds(pl.multiple_of(index * size, size), size)
@@ -512,32 +523,94 @@
             {"seq": partner},
         )
 
-    def gather_ops(i, r, act):
-        act(pair_copy(i, r))
+    n_passed = n_own // 2
+
+    def gather_ops(i, r, act, later=False):
+        if not later:
+            act(pair_copy(i, r))
         for chip_step in range(1, n_chips):
-
-            @pl.when(chip + chip_step < n_chips)
+            mine = chip + chip_step < n_chips
+            if chip_step == 3:
+                mine = mine & (i >= n_passed)
+            if chip_step == 1:
+                mine = mine & ((chip == 1) if later else (chip != 1))
+            elif later:
+                continue
+
+            @pl.when(mine)
             def _():
                 for parity in range(2):
                     act(gather_copy(i, r, parity, chip_step))
 
+    def later_ops(index, act):
+        @pl.when((chip == 1) & (index >= n_passed * n_roll) & (index < n_units))
+        def _():
+            gather_ops(index // n_roll, index % n_roll, act, later=True)
+
+    def gather_got(i, r, device):
+        return remote(
+            kv_own.at[0, r],
+            kv_all.at[i, r, :, seq_rows(device), :],
+            kv_send.at[i, r, 0, 0],
+            kv_recv.at[i, r, device],
+            {"seq": partner},
+        )
+
+    def pass_copy(i, r, source_core):
+        source = 2 * (chip - 2) + source_core
+        return remote(
+            kv_all.at[i, r, :, seq_rows(source), :],
+            kv_all.at[i, r, :, seq_rows(source), :],
+            fw_send.at[i, r, source_core],
+            kv_recv.at[i, r, source],
+            {"seq": 2 * (5 - chip) + core},
+        )
+
+    def pass_on(index, carry):
+        i = index // n_roll
+        r = index % n_roll
+        gather_ops(i, r, lambda copy: copy.start())
+
+        @pl.when(i < n_passed)
+        def _():
+            for source_core in range(2):
+                gather_got(i, r, 2 * (chip - 2) + source_core).wait_recv()
+                pass_copy(i, r, source_core).start()
+
+        return carry
+
+    def passed_sent(i, r):
+        @pl.when((chip >= 2) & (i < n_passed))
+        def _():
+            for source_core in range(2):
+                pass_copy(i, r, source_core).wait_send()
+
     def gather_wait(i, r):
-        def got(device):
-            remote(
-                kv_own.at[0, r],
-                kv_all.at[i, r, :, seq_rows(device), :],
-                kv_send.at[i, r, 0, 0],
-                kv_recv.at[i, r, device],
-                {"seq": partner},
-            ).wait_recv()
-
-        got(partner)
-        for source in range(n_chips - 1):
-
-            @pl.when(source < chip)
-            def _():
-                got(2 * source)
-                got(2 * source + 1)
+        def block(source):
+            for source_core in range(2):
+                gather_got(i, r, 2 * source + source_core).wait_recv()
+
+        gather_got(i, r, partner).wait_recv()
+
+        @pl.when((chip == 1) | ((chip >= 2) & (i >= n_passed)))
+        def _():
+            block(0)
+
+        @pl.when((chip >= 2) & (i >= n_passed))
+        def _():
+            block(1)
+
+        @pl.when((chip == 2) & (i < n_passed))
+        def _():
+            block(1)
+
+        @pl.when((chip == 3) & (i < n_passed))
+        def _():
+            block(0)
+
+        @pl.when(chip == 3)
+        def _():
+            block(2)
 
     def reduce_copy(i, r, target_chip, target_core):
         target = 2 * target_chip + target_core
@@ -549,15 +622,92 @@
             {"seq": target},
         )
 
+    def chip_block(target_chip):
+        return pl.ds(target_chip * chip_tokens, chip_tokens)
+
+    def merge_copy(i, r, target_chip):
+        return remote(
+            dkv_own.at[i, r, :, chip_block(0), :],
+            merge_buf.at[i, r],
+            mg_send.at[i, r],
+            mg_recv.at[i, r],
+            {"seq": 2 * target_chip + core},
+        )
+
+    def relay_copy(i, r):
+        return remote(
+            dkv_own.at[i, r, :, chip_block(1), :],
+            relay_buf.at[i, r],
+            rl_send.at[i, r],
+            rl_recv.at[i, r],
+            {"seq": core},
+        )
+
+    def pass_back_copy(i, r, target_core):
+        return remote(
+            relay_buf.at[i, r, :, pl.ds(target_core * tokens, tokens), :],
+            dkv_all.at[2, 2 * i + core, r],
+            dk_send.at[i, r, 1, target_core],
+            dk_recv.at[2, 2 * i + core, r],
+            {"seq": 2 + target_core},
+        )
+
+    def merges(r):
+        return ((chip == 1) & (r % 2 == 0)) | ((chip == 2) & (r % 2 == 1))
+
+    def block_ops(i, r, target_chip, act):
+        for target_core in range(2):
+            act(reduce_copy(i, r, target_chip, target_core))
+
     def reduce_ops(i, r, act):
-        for target_chip in range(n_chips - 1):
-
-            @pl.when(target_chip < chip)
+        act(reduce_copy(i, r, chip, 1 - core))
+        index = i * n_roll + r
+
+        @pl.when(((chip == 1) | (chip == 2)) & ~merges(r))
+        def _():
+            block_ops(i, r, 0, act)
+
+        @pl.when((chip == 2) & (i < n_passed))
+        def _():
+            act(relay_copy(i, r))
+
+        @pl.when((chip == 3) & (index < n_units - HELD))
+        def _():
+            top_ops(i, r, act)
+
+    def top_ops(i, r, act):
+        for route in range(2):
+
+            @pl.when(r % 2 == route)
             def _():
-                for target_core in range(2):
-                    act(reduce_copy(i, r, target_chip, target_core))
-
-        act(reduce_copy(i, r, chip, 1 - core))
+                act(merge_copy(i, r, 1 + route))
+
+        block_ops(i, r, 2, act)
+        block_ops(i, r, 1, act)
+
+    def held_ops(i, r, act):
+        @pl.when((chip == 2) & (i >= n_passed))
+        def _():
+            block_ops(i, r, 1, act)
+
+        @pl.when((chip == 3) & (i * n_roll + r >= n_units - HELD))
+        def _():
+            top_ops(i, r, act)
+
+    def merge(i, r):
+        @pl.when(merges(r))
+        def _():
+            merge_copy(i, r, 0).wait_recv()
+            for t in range(2):
+                block = dkv_own[i, r, t, :chip_tokens, :].astype(jnp.float32)
+                block = block + merge_buf[i, r, t].astype(jnp.float32)
+                dkv_own[i, r, t, :chip_tokens, :] = block.astype(jnp.bfloat16)
+            block_ops(i, r, 0, lambda copy: copy.start())
+
+    def pass_back(i, r):
+        relay_copy(i, r).wait_recv()
+        for target_core in range(2):
+            pass_back_copy(i, r, target_core).start()
 
     def reduce_got(source, h, r):
         return remote(
@@ -585,8 +735,6 @@
             ad_recv.at[t, source],
             {"seq": 2 * target_chip + core},
         )
-
-    pl.semaphore_wait(barrier, n_seq + n_dp - 2)
 
     k_load.wait()
     cos_load.wait()
@@ -601,12 +749,17 @@
             kv_own[h, r, 0] = key.astype(jnp.bfloat16)
     for h in range(kv_heads):
         v_load(h).wait()
-    each_unit(lambda i, r: gather_ops(i, r, lambda copy: copy.start()))
-    each_unit(send_queries)
-
     for i in range(n_own):
         for r in range(n_roll):
             kv_all[i, r, :, seq_rows(me), :] = kv_own[2 * i + core, r]
+
+    pl.semaphore_wait(barrier, n_seq + n_dp - 2)
+
+    @pl.when(chip < 2)
+    def _():
+        each_unit(lambda i, r: gather_ops(i, r, lambda copy: copy.start()))
+
+    each_unit(send_queries)
 
     hid_load.wait()
     down_load.wait()
@@ -619,6 +772,11 @@
     lat_copy.start()
     for i in range(n_own):
         hid_copy(i).start()
+
+    @pl.when(chip >= 2)
+    def _():
+        lax.fori_loop(0, n_units, pass_on, 0)
+
     back_acc[...] = jnp.zeros_like(back_acc)
     up_acc[...] = jnp.zeros_like(up_acc)
     up_load.wait()
@@ -702,6 +860,7 @@
     def unit(i, r):
         h = 2 * i + core
         gather_wait(i, r)
+        later_ops(i * n_roll + r + SEND_AHEAD, lambda copy: copy.start())
         q_load(i, r).wait()
         g_load(i, r).wait()
         remote(
@@ -726,6 +885,12 @@
 
         reduce_ops(i, r, lambda copy: copy.start())
         gq_copy(i, r, core).start()
+        late = i * n_roll + r - MERGE_LAG
+
+        @pl.when(late >= 0)
+        def _():
+            merge(late // n_roll, late % n_roll)
+
         dkv_all[chip, h, r] = dkv_own[i, r, :, seq_rows(me), :]
         gq_ref[r, :, lanes(h, span)] = gq_all[i, r, core]
         grad_query = gq_all[i, r].reshape(chip_tokens, span)
@@ -825,12 +990,22 @@
         for d in range(n_dp):
             out[:, d * piece : (d + 1) * piece] = z_all[t, d].astype(jnp.float32)
 
+    each_unit(lambda i, r: held_ops(i, r, lambda copy: copy.start()))
+
+    @pl.when(chip == 0)
+    def _():
+        for i in range(n_passed):
+            for r in range(n_roll):
+                pass_back(i, r)
+
     owner_sum(1, up_own, up_got)
     scatter_start(1)
 
     cos_own = cos_ref[own_rows, :]
     sin_own = sin_ref[own_rows, :]
 
+    n_sources = jnp.where(chip == 0, n_chips - 1, n_chips)
+
     def finish(h, r):
         @pl.when(h % 2 != core)
         def _():
@@ -838,7 +1013,7 @@
 
         for source in range(1, n_chips):
 
-            @pl.when(source > chip)
+            @pl.when((source > chip) & (source < n_sources))
             def _():
                 reduce_got(source, h, r).wait_recv()
 
@@ -848,7 +1023,7 @@
             )
 
         first = tuple(dkv_all[chip, h, r, t].astype(jnp.float32) for t in range(2))
-        key, value = lax.fori_loop(chip + 1, n_chips, add, first)
+        key, value = lax.fori_loop(chip + 1, n_sources, add, first)
         key = key * cos_own - pltpu.roll(key, half, 1) * sin_own
         gk_ref[r, :, lanes(h, width)] = key.astype(jnp.bfloat16)
         gv_ref[r, :, lanes(h, width)] = value.astype(jnp.bfloat16)
@@ -857,8 +1032,8 @@
         finish(index // n_roll, index % n_roll)
         return carry
 
-    lax.fori_loop(0, kv_heads * n_roll, finish_step, 0)
-
+    early = (kv_heads - 4) * n_roll
+    lax.fori_loop(0, early, finish_step, 0)
     collect_start(1)
     owner_sum(0, dn_own, dn_got)
     scatter_start(0)
@@ -866,8 +1041,31 @@
     each_unit(lambda i, r: gq_copy(i, r, 1 - core).wait_recv())
     collect_start(0)
 
+    def merge_step(index, carry):
+        merge(index // n_roll, index % n_roll)
+        return carry
+
+    lax.fori_loop(max(0, n_units - MERGE_LAG), n_units, merge_step, 0)
+
+    lax.fori_loop(early, kv_heads * n_roll, finish_step, 0)
+
     each_unit(lambda i, r: gather_ops(i, r, lambda copy: copy.wait_send()))
+    each_unit(lambda i, r: later_ops(i * n_roll + r, lambda copy: copy.wait_send()))
     each_unit(lambda i, r: reduce_ops(i, r, lambda copy: copy.wait_send()))
+    each_unit(lambda i, r: held_ops(i, r, lambda copy: copy.wait_send()))
+    each_unit(passed_sent)
+
+    def merged_sent(i, r):
+        @pl.when(merges(r))
+        def _():
+            block_ops(i, r, 0, lambda copy: copy.wait_send())
+
+        @pl.when((chip == 0) & (i < n_passed))
+        def _():
+            for target_core in range(2):
+                pass_back_copy(i, r, target_core).wait_send()
+
+    each_unit(merged_sent)
 
     def sent(i, r):
         q_copy(i, r).wait_send()
@@ -936,7 +1134,7 @@
     full = jnp.float32
     dma = pltpu.SemaphoreType.DMA
     vm = pltpu.VMEM
-    anywhere = pl.BlockSpec(memory_space=pl.ANY)
+    anywhere = pl.BlockSpec(memory_space=pltpu.HBM)
     vmem = pl.BlockSpec(memory_space=pltpu.VMEM)
     out_types = [
         ((n_roll, tokens, q_width), low),
@@ -981,6 +1179,8 @@
             vm((2, rank, span), low),
             vm((2, n_dp, rank, span // n_dp), low),
             vm((2, n_dp, rank, span // n_dp), low),
+            vm((n_own, n_roll, 2, 2 * tokens, HEAD_WIDTH), low),
+            vm((n_own, n_roll, 2, 2 * tokens, HEAD_WIDTH), low),
             dma((8,)),
             dma((kv_heads,)),
             dma((n_own, n_roll)),
@@ -1005,22 +1205,32 @@
             dma((2, n_dp)),
             dma((2, n_dp)),
             dma((2, n_dp)),
+            dma((n_own, n_roll, 2)),
+            dma((n_own, n_roll)),
+            dma((n_own, n_roll)),
+            dma((n_own, n_roll)),
+            dma((n_own, n_roll)),
         ],
         compiler_params=pltpu.CompilerParams(
             collective_id=0, has_side_effects=True, vmem_limit_bytes=VMEM_LIMIT
         ),
     )(
-        offsets,
-        lengths,
-        jnp.asarray(cos_wide),
-        jnp.asarray(sin_wide),
-        queries,
-        unrotated_key_rows,
-        value_projection_rows,
-        attention_output_gradient,
-        normed_hidden_input,
-        adapter_down_weight.T,
-        adapter_up_weight,
+        *[
+            pltpu.with_memory_space_constraint(value, pltpu.HBM)
+            for value in (
+                offsets,
+                lengths,
+                jnp.asarray(cos_wide),
+                jnp.asarray(sin_wide),
+                queries,
+                unrotated_key_rows,
+                value_projection_rows,
+                attention_output_gradient,
+                normed_hidden_input,
+                adapter_down_weight.T,
+                adapter_up_weight,
+            )
+        ]
     )
     outs = pl.pallas_call(
         partial(write_kernel, len(out_types)),
@@ -1046,7 +1256,7 @@
     held = 3 * 2 * n_roll * length * kv_width + 10 * n_roll * tokens * q_width
     held = held + 12 * length * rows
     fits = held < VMEM_LIMIT // 2
-    whole = kv_heads == n_seq and n_seq % 2 == 0 and 2 * tokens == HEAD_WIDTH
+    whole = kv_heads == n_seq and n_seq == 8 and 2 * tokens == HEAD_WIDTH
     whole = whole and 2 * tokens >= OFFSET_BOUND and (group * HEAD_WIDTH) % (n_dp * 128) == 0
     if not (fits and whole):
         return on_device(*args)

time: 68.4 us -> 55.4 us (0.81)
  local copies, waits for them, and re-layouts: 8.98 us -> 0 us
  Pallas kernels: 58.3 us -> 54.6 us
    unnamed x20 -> x0, local copies, waits for them, and re-layouts: 8.98 us -> none
    pallas_call x1, Pallas kernels: 57 us -> 53.3 us  [fused_on_device(): pl.pallas_call(partial(fused_kernel, n_seq, n_dp, n_roll, tokens, kv_head...]
where the time goes in v2:
time: 55.4 us; the launch traced here: 55.2 us
  Pallas kernels  54.6 us (99%)
  between operations  0.64 us (1%)
    pallas_call x1, Pallas kernels, fused_on_device(): pl.pallas_call(partial(fused_kernel, n_seq, n_dp, n_roll, tokens, kv_head...  53.3 us
    pallas_call x1, Pallas kernels, fused_on_device(): pl.pallas_call(partial(write_kernel, len(out_types)), out_shape=[jax.Shap...  1.26 us

profile of v2, /device:TPU:0, one launch (start us, length us, event | category | flops | bytes accessed | tf_op | source)
XLA Modules:
  0.0 55.2 jit_solution(15892367280902401369)
XLA Ops:
  0.6 53.3 %shard_map.146 = (bf16[2,64,4096]{2,1,0:T(8,128)(2,1)S(1)}, bf16[2,64,1024]{2,1,0:T(8,128)(2,1)S(1)}, bf16[2,64,1024]{2,1,0:T(8,128)(2,1)S(1)}, f32[64,512]{1,0:T(8,128)S(1)}, f32[64,512]{1,0:T(8,128)S(1)}) custom-call(s32[2]{0:T(128)} %off_hbm.1, s32[2]{0:T(128)} %len_hbm.1, f32[512,128]{1,0:T(8,128)} %constant.4.clone.cos_hbm, ...), custom_call_target="tpu_custom_call" | custom-call | tf_op jit(solution)/shard_map/pallas_call | solution.py:1146
  54.0 1.3 %shard_map.147 = (bf16[2,64,4096]{2,1,0:T(8,128)(2,1)}, bf16[2,64,1024]{2,1,0:T(8,128)(2,1)}, bf16[2,64,1024]{2,1,0:T(8,128)(2,1)}, f32[64,512]{1,0:T(8,128)}, f32[64,512]{1,0:T(8,128)}) custom-call(bf16[2,64,4096]{2,1,0:T(8,128)(2,1)S(1)} %get-tuple-element.15.refs_0_, bf16[2,64,1024]{2,1,0:T(8,128)(2,1)S(1)} %get-tuple-element.16.refs_1_, ...), custom_call_target="tpu_custom_call" | custom-call | tf_op jit(solution)/shard_map/pallas_call | solution.py:1235

commit v3 on v2

--- a/solution.py
+++ b/solution.py
@@ -291,6 +291,7 @@
 VMEM_LIMIT = 48 * 1024 * 1024
 MERGE_LAG = 3
 HELD = 3
+RELAYED = 5
 SEND_AHEAD = 2
 NEG = -1e30
 OFFSET_BOUND = 32
@@ -667,7 +668,7 @@
         def _():
             block_ops(i, r, 0, act)
 
-        @pl.when((chip == 2) & (i < n_passed))
+        @pl.when((chip == 2) & (index < RELAYED))
         def _():
             act(relay_copy(i, r))
 
@@ -675,24 +676,28 @@
         def _():
             top_ops(i, r, act)
 
+    def to_merge_ops(i, r, act):
+        act(merge_copy(i, r, 1 + r % 2))
+
     def top_ops(i, r, act):
-        for route in range(2):
-
-            @pl.when(r % 2 == route)
-            def _():
-                act(merge_copy(i, r, 1 + route))
-
+        to_merge_ops(i, r, act)
         block_ops(i, r, 2, act)
         block_ops(i, r, 1, act)
 
-    def held_ops(i, r, act):
-        @pl.when((chip == 2) & (i >= n_passed))
-        def _():
-            block_ops(i, r, 1, act)
-
-        @pl.when((chip == 3) & (i * n_roll + r >= n_units - HELD))
-        def _():
-            top_ops(i, r, act)
+    def held_ops(act):
+        @pl.when(chip == 2)
+        def _():
+            for index in range(RELAYED, n_units):
+                block_ops(*divmod(index, n_roll), 1, act)
+
+        @pl.when(chip == 3)
+        def _():
+            held = [divmod(index, n_roll) for index in range(n_units - HELD, n_units)]
+            for i, r in held:
+                to_merge_ops(i, r, act)
+            for i, r in held:
+                block_ops(i, r, 1, act)
+                block_ops(i, r, 2, act)
 
     def merge(i, r):
         @pl.when(merges(r))
@@ -990,13 +995,12 @@
         for d in range(n_dp):
             out[:, d * piece : (d + 1) * piece] = z_all[t, d].astype(jnp.float32)
 
-    each_unit(lambda i, r: held_ops(i, r, lambda copy: copy.start()))
+    held_ops(lambda copy: copy.start())
 
     @pl.when(chip == 0)
     def _():
-        for i in range(n_passed):
-            for r in range(n_roll):
-                pass_back(i, r)
+        for index in range(RELAYED):
+            pass_back(*divmod(index, n_roll))
 
     owner_sum(1, up_own, up_got)
     scatter_start(1)
@@ -1037,22 +1041,24 @@
     collect_start(1)
     owner_sum(0, dn_own, dn_got)
     scatter_start(0)
+
+    def merge_step(index, carry):
+        merge(index // n_roll, index % n_roll)
+        return carry
+
+    lax.fori_loop(max(0, n_units - MERGE_LAG), n_units, merge_step, 0)
+
     collect_out(1, gu_ref)
     each_unit(lambda i, r: gq_copy(i, r, 1 - core).wait_recv())
     collect_start(0)
 
-    def merge_step(index, carry):
-        merge(index // n_roll, index % n_roll)
-        return carry
-
-    lax.fori_loop(max(0, n_units - MERGE_LAG), n_units, merge_step, 0)
 
     lax.fori_loop(early, kv_heads * n_roll, finish_step, 0)
 
     each_unit(lambda i, r: gather_ops(i, r, lambda copy: copy.wait_send()))
     each_unit(lambda i, r: later_ops(i * n_roll + r, lambda copy: copy.wait_send()))
     each_unit(lambda i, r: reduce_ops(i, r, lambda copy: copy.wait_send()))
-    each_unit(lambda i, r: held_ops(i, r, lambda copy: copy.wait_send()))
+    held_ops(lambda copy: copy.wait_send())
     each_unit(passed_sent)
 
     def merged_sent(i, r):
@@ -1060,7 +1066,7 @@
         def _():
             block_ops(i, r, 0, lambda copy: copy.wait_send())
 
-        @pl.when((chip == 0) & (i < n_passed))
+        @pl.when((chip == 0) & (i * n_roll + r < RELAYED))
         def _():
             for target_core in range(2):
                 pass_back_copy(i, r, target_core).wait_send()

time: 55.4 us -> 51.5 us (0.930)
  Pallas kernels: 54.6 us -> 50.7 us
    pallas_call x1, Pallas kernels: 53.3 us -> 49.4 us  [fused_on_device(): pl.pallas_call(partial(fused_kernel, n_seq, n_dp, n_roll, tokens, kv_head...]
where the time goes in v3:
time: 51.5 us; the launch traced here: 51.3 us
  Pallas kernels  50.7 us (98%)
  between operations  0.64 us (1%)
    pallas_call x1, Pallas kernels, fused_on_device(): pl.pallas_call(partial(fused_kernel, n_seq, n_dp, n_roll, tokens, kv_head...  49.4 us
    pallas_call x1, Pallas kernels, fused_on_device(): pl.pallas_call(partial(write_kernel, len(out_types)), out_shape=[jax.Shap...  1.26 us

profile of v3, /device:TPU:0, one launch (start us, length us, event | category | flops | bytes accessed | tf_op | source)
XLA Modules:
  0.0 51.3 jit_solution(8509210409954627255)
XLA Ops:
  0.6 49.4 %shard_map.146 = (bf16[2,64,4096]{2,1,0:T(8,128)(2,1)S(1)}, bf16[2,64,1024]{2,1,0:T(8,128)(2,1)S(1)}, bf16[2,64,1024]{2,1,0:T(8,128)(2,1)S(1)}, f32[64,512]{1,0:T(8,128)S(1)}, f32[64,512]{1,0:T(8,128)S(1)}) custom-call(s32[2]{0:T(128)} %off_hbm.1, s32[2]{0:T(128)} %len_hbm.1, f32[512,128]{1,0:T(8,128)} %constant.4.clone.cos_hbm, ...), custom_call_target="tpu_custom_call" | custom-call | tf_op jit(solution)/shard_map/pallas_call | solution.py:1152
  50.1 1.3 %shard_map.147 = (bf16[2,64,4096]{2,1,0:T(8,128)(2,1)}, bf16[2,64,1024]{2,1,0:T(8,128)(2,1)}, bf16[2,64,1024]{2,1,0:T(8,128)(2,1)}, f32[64,512]{1,0:T(8,128)}, f32[64,512]{1,0:T(8,128)}) custom-call(bf16[2,64,4096]{2,1,0:T(8,128)(2,1)S(1)} %get-tuple-element.15.refs_0_, bf16[2,64,1024]{2,1,0:T(8,128)(2,1)S(1)} %get-tuple-element.16.refs_1_, ...), custom_call_target="tpu_custom_call" | custom-call | tf_op jit(solution)/shard_map/pallas_call | solution.py:1241
